TPU v7x, 32 devices: a whole 2x2x4 slice. The times are simulated.
32 devices in a mesh: tp: 4 (over z), cp: 8 (over y, x, core).
Axes of the slice: x: 2, y: 2, z: 4, core: 2. Of those that a mesh axis runs over, the one named last changes fastest.
Arguments:
- x_in: bfloat16 [1, 3072, 5120], P(None, 'cp')
- positions: int32 [3072], P('cp')
- rope_cos: float32 [3072, 128], P('cp')
- rope_sin: float32 [3072, 128], P('cp')
- norm_a: bfloat16 [5120], replicated
- wq_a: bfloat16 [5120, 5120], P(None, 'tp')
- wk_a: bfloat16 [5120, 1024], P(None, 'tp')
- wv_a: bfloat16 [5120, 1024], P(None, 'tp')
- wo_a: bfloat16 [5120, 5120], P('tp')
- norm_b: bfloat16 [5120], replicated
- wq_b: bfloat16 [5120, 5120], P(None, 'tp')
- wk_b: bfloat16 [5120, 1024], P(None, 'tp')
- wv_b: bfloat16 [5120, 1024], P(None, 'tp')
- wo_b: bfloat16 [5120, 5120], P('tp')
- grad_y: bfloat16 [1, 3072, 5120], P(None, 'cp')
Outputs:
- output 1: bfloat16 [1, 3072, 5120], P(None, 'cp')
- output 2: bfloat16 [1, 3072, 5120], P(None, 'cp')
- output 3: bfloat16 [5120], P('cp')
- output 4: bfloat16 [5120, 5120], P('cp', 'tp')
- output 5: bfloat16 [5120, 1024], P('cp', 'tp')
- output 6: bfloat16 [5120, 1024], P('cp', 'tp')
- output 7: bfloat16 [5120, 5120], P(('tp', 'cp'))
- output 8: bfloat16 [5120], P('cp')
- output 9: bfloat16 [5120, 5120], P('cp', 'tp')
- output 10: bfloat16 [5120, 1024], P('cp', 'tp')
- output 11: bfloat16 [5120, 1024], P('cp', 'tp')
- output 12: bfloat16 [5120, 5120], P(('tp', 'cp'))
All inputs are finite; a program needn't handle non-finite values.
Results may differ from a plain program's by a relative error of at most 0.02.
Values are sent between devices in bfloat16 or wider.
A program may use at most 1 GiB of HBM per device.

v0:
```python
import jax
import jax.numpy as jnp
from jax import lax
from jax.sharding import PartitionSpec as P

CHUNK = 8192
NORM_EPS = 1e-5
QK_EPS = 1e-6
TEMP_SCALE = 0.1
NEG_BIG = -1e30


def rms_norm(act, gamma):
    act_wide = act.astype(jnp.float32)
    inv_rms = lax.rsqrt(jnp.mean(act_wide * act_wide, axis=-1, keepdims=True) + NORM_EPS)
    return (act_wide * inv_rms * gamma.astype(jnp.float32)).astype(jnp.bfloat16)


def norm_backward(act, gamma, grad_out):
    act_wide = act.astype(jnp.float32)
    inv_rms = lax.rsqrt(jnp.mean(act_wide * act_wide, axis=-1, keepdims=True) + NORM_EPS)
    x_hat = act_wide * inv_rms
    grad_gain = jnp.sum(grad_out * x_hat, axis=(0, 1))
    grad_hat = grad_out * gamma.astype(jnp.float32)
    grad_act = inv_rms * (grad_hat - x_hat * jnp.mean(grad_hat * x_hat, axis=-1, keepdims=True))
    return grad_act, grad_gain


def rotate(wide, cos_tab, sin_tab):
    half = wide.shape[-1] // 2
    turned = jnp.concatenate([-wide[..., half:], wide[..., :half]], axis=-1)
    return wide * cos_tab[None, :, None, :] + turned * sin_tab[None, :, None, :]


def qk_prep(raw_val, cos_tab, sin_tab):
    wide = rotate(raw_val.astype(jnp.float32), cos_tab, sin_tab)
    return (wide * lax.rsqrt(jnp.mean(wide * wide, axis=-1, keepdims=True) + QK_EPS)).astype(jnp.bfloat16)


def value_a11(positions):
    return jnp.log(((positions + 1) // CHUNK).astype(jnp.float32) + 1.0) * TEMP_SCALE + 1.0


def project(act, weight):
    return jnp.einsum('bsd,dh->bsh', act, weight, preferred_element_type=jnp.float32).astype(jnp.bfloat16)


def project_back(grad_out, weight):
    return jnp.einsum('bsh,dh->bsd', grad_out, weight, preferred_element_type=jnp.float32)


def weight_grad(act, grad_out):
    return jnp.einsum('bsd,bsh->dh', act, grad_out, preferred_element_type=jnp.float32)


def attn_forward(queries, keys, values, allowed, scale):
    scores = jnp.einsum('bqkgd,bskd->bkgqs', queries, keys, preferred_element_type=jnp.float32) * scale
    attn_prob = jax.nn.softmax(jnp.where(allowed, scores, NEG_BIG), axis=-1)
    prob_half = attn_prob.astype(jnp.bfloat16)
    attn_out = jnp.einsum('bkgqs,bskd->bqkgd', prob_half, values, preferred_element_type=jnp.float32)
    return attn_out.astype(jnp.bfloat16), attn_prob, prob_half


def attn_backward(queries, keys, values, attn_prob, prob_half, grad_out, scale):
    grad_value = jnp.einsum('bkgqs,bqkgd->bskd', prob_half, grad_out, preferred_element_type=jnp.float32)
    grad_prob = jnp.einsum('bqkgd,bskd->bkgqs', grad_out, values, preferred_element_type=jnp.float32)
    row_dot = jnp.sum(attn_prob * grad_prob, axis=-1, keepdims=True)
    grad_score = (attn_prob * (grad_prob - row_dot) * scale).astype(jnp.bfloat16)
    grad_query = jnp.einsum('bkgqs,bskd->bqkgd', grad_score, keys, preferred_element_type=jnp.float32)
    grad_key = jnp.einsum('bkgqs,bqkgd->bskd', grad_score, queries, preferred_element_type=jnp.float32)
    return grad_query, grad_key, grad_value


def solution(mesh):
    cp_size = mesh.shape['cp']
    row_spec = P(None, 'cp', None)
    col_spec = P(None, 'tp')
    grid_spec = P('cp', 'tp')
    out_rows = P(('tp', 'cp'), None)
    in_specs = (row_spec, P('cp'), P('cp', None), P('cp', None),
                P(None), col_spec, col_spec, col_spec, P('tp', None),
                P(None), col_spec, col_spec, col_spec, P('tp', None), row_spec)
    out_specs = (row_spec, row_spec,
                 P('cp'), grid_spec, grid_spec, grid_spec, out_rows,
                 P('cp'), grid_spec, grid_spec, grid_spec, out_rows)

    def body(x_in, positions, rope_cos, rope_sin, norm_a, wq_a, wk_a, wv_a, wo_a,
             norm_b, wq_b, wk_b, wv_b, wo_b, grad_y):
        batch, block = x_in.shape[0], x_in.shape[1]
        head_dim = rope_cos.shape[1]
        q_local = wq_a.shape[1] // head_dim
        kv_local = wk_a.shape[1] // head_dim
        q_shape = (batch, block, kv_local, q_local // kv_local, head_dim)
        kv_shape = (batch, block, kv_local, head_dim)
        flat_shape = (batch, block, -1)
        scale = head_dim ** -0.5
        cp_rank = lax.axis_index('cp')
        n_back = min(cp_size - 1, (CHUNK + block - 2) // block)
        window = (n_back + 1) * block
        seq_len = block * cp_size

        def prep(raw_val):
            return qk_prep(raw_val, rope_cos, rope_sin)

        xn_a = rms_norm(x_in, norm_a)
        q_prepped, q_pull = jax.vjp(prep, project(xn_a, wq_a).reshape(batch, block, q_local, head_dim))
        query_a = q_prepped.reshape(q_shape)
        key_a, k_pull = jax.vjp(prep, project(xn_a, wk_a).reshape(kv_shape))
        value_a = project(xn_a, wv_a).reshape(kv_shape)
        key_parts = []
        value_parts = []
        for shift in range(n_back, 0, -1):
            fwd_perm = [(source, source + shift) for source in range(cp_size - shift)]
            key_parts.append(lax.ppermute(key_a, 'cp', fwd_perm))
            value_parts.append(lax.ppermute(value_a, 'cp', fwd_perm))
        key_win = jnp.concatenate(key_parts + [key_a], axis=1)
        value_win = jnp.concatenate(value_parts + [value_a], axis=1)
        offsets = jnp.arange(window) - n_back * block
        key_pos = positions[0] + offsets
        allowed_a = ((key_pos[None, :] <= positions[:, None])
                     & ((key_pos // CHUNK)[None, :] == (positions // CHUNK)[:, None])
                     & (cp_rank * block + offsets >= 0)[None, :])
        out_a, prob_a, half_a = attn_forward(query_a, key_win, value_win, allowed_a, scale)
        out_a = out_a.reshape(flat_shape)
        attn_a = lax.psum(project(out_a, wo_a), 'tp')
        h_mid = (x_in.astype(jnp.float32) + attn_a.astype(jnp.float32)).astype(jnp.bfloat16)

        xn_b = rms_norm(h_mid, norm_b)
        q_temp = value_a11(positions)[None, :, None]
        query_b = (project(xn_b, wq_b).astype(jnp.float32) * q_temp).astype(jnp.bfloat16).reshape(q_shape)
        key_b = project(xn_b, wk_b).reshape(kv_shape)
        value_b = project(xn_b, wv_b).reshape(kv_shape)
        key_all = lax.all_gather(key_b, 'cp', axis=1, tiled=True)
        value_all = lax.all_gather(value_b, 'cp', axis=1, tiled=True)
        allowed_b = jnp.arange(seq_len)[None, :] <= (cp_rank * block + jnp.arange(block))[:, None]
        out_b, prob_b, half_b = attn_forward(query_b, key_all, value_all, allowed_b, scale)
        out_b = out_b.reshape(flat_shape)
        attn_b = lax.psum(project(out_b, wo_b), 'tp')
        out_y = (h_mid.astype(jnp.float32) + attn_b.astype(jnp.float32)).astype(jnp.bfloat16)

        grad_wo_b = weight_grad(out_b, grad_y)
        grad_ob = project_back(grad_y, wo_b).astype(jnp.bfloat16).reshape(q_shape)
        grad_q_b, grad_k_all, grad_v_all = attn_backward(query_b, key_all, value_all, prob_b, half_b, grad_ob, scale)
        grad_k_b = lax.psum_scatter(grad_k_all.astype(jnp.bfloat16), 'cp', scatter_dimension=1, tiled=True).reshape(flat_shape)
        grad_v_b = lax.psum_scatter(grad_v_all.astype(jnp.bfloat16), 'cp', scatter_dimension=1, tiled=True).reshape(flat_shape)
        grad_q_b = (grad_q_b.reshape(flat_shape) * q_temp).astype(jnp.bfloat16)
        grad_wq_b = weight_grad(xn_b, grad_q_b)
        grad_wk_b = weight_grad(xn_b, grad_k_b)
        grad_wv_b = weight_grad(xn_b, grad_v_b)
        grad_xn_b = project_back(grad_q_b, wq_b) + project_back(grad_k_b, wk_b) + project_back(grad_v_b, wv_b)
        grad_xn_b = lax.psum(grad_xn_b.astype(jnp.bfloat16), 'tp')
        grad_h_norm, grad_norm_b = norm_backward(h_mid, norm_b, grad_xn_b.astype(jnp.float32))
        grad_h = (grad_y.astype(jnp.float32) + grad_h_norm).astype(jnp.bfloat16)

        grad_wo_a = weight_grad(out_a, grad_h)
        grad_oa = project_back(grad_h, wo_a).astype(jnp.bfloat16).reshape(q_shape)
        grad_q_a, grad_k_win, grad_v_win = attn_backward(query_a, key_win, value_win, prob_a, half_a, grad_oa, scale)
        grad_k_own = grad_k_win[:, n_back * block:]
        grad_v_own = grad_v_win[:, n_back * block:]
        send_k = grad_k_win[:, :n_back * block].astype(jnp.bfloat16)
        send_v = grad_v_win[:, :n_back * block].astype(jnp.bfloat16)
        for shift in range(1, n_back + 1):
            back_perm = [(source, source - shift) for source in range(shift, cp_size)]
            start_row = (n_back - shift) * block
            grad_k_own = grad_k_own + lax.ppermute(send_k[:, start_row:start_row + block], 'cp', back_perm).astype(jnp.float32)
            grad_v_own = grad_v_own + lax.ppermute(send_v[:, start_row:start_row + block], 'cp', back_perm).astype(jnp.float32)
        grad_q_raw = q_pull(grad_q_a.astype(jnp.bfloat16).reshape(batch, block, q_local, head_dim))[0].reshape(flat_shape)
        grad_k_raw = k_pull(grad_k_own.astype(jnp.bfloat16))[0].reshape(flat_shape)
        grad_v_raw = grad_v_own.astype(jnp.bfloat16).reshape(flat_shape)
        grad_wq_a = weight_grad(xn_a, grad_q_raw)
        grad_wk_a = weight_grad(xn_a, grad_k_raw)
        grad_wv_a = weight_grad(xn_a, grad_v_raw)
        grad_xn_a = project_back(grad_q_raw, wq_a) + project_back(grad_k_raw, wk_a) + project_back(grad_v_raw, wv_a)
        grad_xn_a = lax.psum(grad_xn_a.astype(jnp.bfloat16), 'tp')
        grad_x_norm, grad_norm_a = norm_backward(x_in, norm_a, grad_xn_a.astype(jnp.float32))
        grad_x = (grad_h.astype(jnp.float32) + grad_x_norm).astype(jnp.bfloat16)

        def to_rows(part):
            return lax.psum_scatter(part, 'cp', scatter_dimension=0, tiled=True).astype(jnp.bfloat16)

        return (out_y, grad_x,
                to_rows(grad_norm_a), to_rows(grad_wq_a), to_rows(grad_wk_a), to_rows(grad_wv_a), to_rows(grad_wo_a),
                to_rows(grad_norm_b), to_rows(grad_wq_b), to_rows(grad_wk_b), to_rows(grad_wv_b), to_rows(grad_wo_b))

    return jax.shard_map(body, mesh=mesh, in_specs=in_specs, out_specs=out_specs, check_vma=False)
```

profile of v0, /device:TPU:0, one launch (start us, length us, event | category | flops | bytes accessed | tf_op | source)
XLA Modules:
  0.0 2015.1 jit_solution(15358477847970894100)
XLA Ops:
  11.1 4.7 convolution_convert_fusion.6
  18.3 6.1 collective-permute-start.7
  30.3 5.3 convolution_convert_fusion.7
  39.5 11.9 fusion.89
  59.3 4.2 and_and_fusion
  63.5 3.5 fusion.92
  79.1 3.5 collective-permute-start.3
  89.0 5.8 collective-permute-done.3
  100.6 20.3 %fusion.12 = (f32[2,5,384]{2,1,0:T(8,128)S(1)}, f32[2,3072,384,5]{2,1,3,0:T(8,128)}) fusion(pred[384,3072]{0,1:T(8,128)(4,1)} %and_and_fusion, bf16[384,2,5,128]{0,3,2,1:T(8,128)(2,1)} %fusion.92, bf16[1,3072,2,128]{3,1,2,0:T(8,128)(2,1)} %copy-done.29), kind=kOutput, calls=%fused_computation.20 | convolution fusion | flops 3055284480 | bytes 50936832 | tf_op jit(solution)/shard_map/bqkgd,bskd->bkgqs/dot_general | solution.py:57
  120.9 20.6 %fusion.9 = f32[2,5,384]{2,1,0:T(8,128)S(1)} fusion(f32[2,3072,384,5]{2,1,3,0:T(8,128)} %get-tuple-element.51, f32[2,5,384]{2,1,0:T(8,128)S(1)} %get-tuple-element.50, pred[384,3072]{0,1:T(8,128)(4,1)} %and_and_fusion), kind=kLoop, calls=%fused_computation.17 | loop fusion | flops 47182080 | bytes 48396288 | tf_op jit(solution)/shard_map/reduce_sum | solution.py:58
  141.5 21.3 %fusion.112 = bf16[2,128,5,384]{3,1,2,0:T(8,128)(2,1)S(1)} fusion(bf16[1,3072,2,128]{1,3,2,0:T(8,128)(2,1)} %constant_dynamic-update-slice_fusion, f32[2,5,384]{2,1,0:T(8,128)S(1)} %fusion.9, f32[2,5,384]{2,1,0:T(8,128)S(1)} %get-tuple-element.50, f32[2,3072,384,5]{2,1,3,0:T(8,128)} %get-tuple-element.51, pred[384,3072]{0,1:T(8,128)(4,1)S(1)} %copy-done.15), kind=kOutput, calls=%fused_computation.134 | convolution fusion | flops 3079372800 | bytes 50952192 | tf_op jit(solution)/shard_map/bkgqs,bskd->bqkgd/dot_general | solution.py:60
  163.8 11.6 fusion.52
  176.0 15.0 fusion.80
  191.0 133.2 %all-reduce.12.cloned.1.call-done = bf16[1,384,5120]{2,1,0:T(8,128)(2,1)} async-done(((bf16[1,384,5120]{2,1,0:T(8,128)(2,1)}), bf16[1,384,5120]{2,1,0:T(8,128)(2,1)}) %all-reduce.12.cloned.1.call-update) | async-done | bytes 3932176 | tf_op jit(solution)/shard_map/psum | solution.py:125
  324.2 5.1 fusion.50
  336.3 11.9 fusion.88
  350.6 5.3 convolution_convert_fusion.5
  356.8 20.8 %fusion.13 = (f32[2,5,384]{2,1,0:T(8,128)S(1)}, f32[2,3072,384,5]{2,1,3,0:T(8,128)}) fusion(pred[384,3072]{0,1:T(8,128)(4,1)} %iota_compare_fusion, bf16[384,2,5,128]{0,3,2,1:T(8,128)(2,1)} %bitcast.356, bf16[1,3072,2,128]{3,1,2,0:T(8,128)(2,1)} %all-gather.5.cloned.1.call-done), kind=kOutput, calls=%fused_computation.21 | convolution fusion | flops 3055284480 | bytes 50936832 | tf_op jit(solution)/shard_map/bqkgd,bskd->bkgqs/dot_general | solution.py:57
  377.6 19.5 fusion.11
  397.1 36.5 %fusion.4 = (f32[2,5,384]{2,1,0:T(8,128)S(1)}, f32[2,3072,384,5]{2,1,3,0:T(8,128)}) fusion(f32[2,5,384]{2,1,0:T(8,128)S(1)} %fusion.11, f32[2,5,384]{2,1,0:T(8,128)S(1)} %get-tuple-element.52, f32[2,3072,384,5]{2,1,3,0:T(8,128)} %get-tuple-element.53, pred[384,3072]{0,1:T(8,128)(4,1)} %iota_compare_fusion, bf16[384,2,5,128]{0,3,2,1:T(8,128)(2,1)} %bitcast.380, ...), kind=kOutput, calls=%fused_computation.10 | convolution fusion | flops 3090673920 | bytes 98153472 | tf_op jit(solution)/shard_map/bqkgd,bskd->bkgqs/dot_general | solution.py:66
  433.6 38.3 %fusion.14 = bf16[2,5,384,3072]{2,3,1,0:T(8,128)(2,1)} fusion(f32[2,3072,384,5]{2,1,3,0:T(8,128)} %get-tuple-element.55, f32[2,5,384]{2,1,0:T(8,128)S(1)} %get-tuple-element.54, f32[2,5,384]{2,1,0:T(8,128)S(1)} %fusion.11, f32[2,5,384]{2,1,0:T(8,128)S(1)} %get-tuple-element.52, f32[2,3072,384,5]{2,1,3,0:T(8,128)} %get-tuple-element.53, ...), kind=kLoop, calls=%fused_computation.22 | loop fusion | flops 94371840 | bytes 119190528 | tf_op jit(solution)/shard_map/reshape.83
  472.0 13.5 fusion.76
  485.5 4.9 copy.157
  493.2 21.9 %fusion.77 = bf16[1,3072,2,128]{1,3,2,0:T(8,128)(2,1)} fusion(bf16[384,2,5,128]{0,3,2,1:T(8,128)(2,1)} %bitcast.381, f32[2,5,384]{2,1,0:T(8,128)S(1)} %fusion.11, f32[2,5,384]{2,1,0:T(8,128)S(1)} %get-tuple-element.52, f32[2,3072,384,5]{2,1,3,0:T(8,128)} %get-tuple-element.53, pred[384,3072]{0,1:T(8,128)(4,1)} %iota_compare_fusion), kind=kOutput, calls=%fused_computation.95 | convolution fusion | flops 3079667712 | bytes 50952192 | tf_op jit(solution)/shard_map/bkgqs,bqkgd->bskd/dot_general | solution.py:65
  515.1 13.4 fusion.94
  531.4 4.9 copy.159
  539.2 16.2 fusion.128
  556.5 4.5 fusion.194
  560.9 16.7 reduce-scatter.33.cloned.1.call-done
  578.8 9.6 fusion.54
  588.5 6.5 fusion.177
  596.3 20.9 %fusion.117 = bf16[2,128,5,384]{3,1,2,0:T(8,128)(2,1)S(1)} fusion(bf16[1,3072,2,128]{1,3,2,0:T(8,128)(2,1)} %all-gather.3.cloned.1.call-done, f32[2,5,384]{2,1,0:T(8,128)S(1)} %fusion.11, f32[2,5,384]{2,1,0:T(8,128)S(1)} %get-tuple-element.52, f32[2,3072,384,5]{2,1,3,0:T(8,128)} %get-tuple-element.53, pred[384,3072]{0,1:T(8,128)(4,1)S(1)} %copy-done.18), kind=kOutput, calls=%fused_computation.135 | convolution fusion | flops 3079372800 | bytes 50952192 | tf_op jit(solution)/shard_map/bkgqs,bskd->bqkgd/dot_general | solution.py:60
  617.2 12.1 fusion.53
  629.3 4.3 fusion.175
  633.7 101.4 %all-reduce.14.cloned.1.call-done = bf16[1,384,5120]{2,1,0:T(8,128)(2,1)} async-done(((bf16[1,384,5120]{2,1,0:T(8,128)(2,1)}), bf16[1,384,5120]{2,1,0:T(8,128)(2,1)}) %all-reduce.14.cloned.1.call-update) | async-done | bytes 3932176 | tf_op jit(solution)/shard_map/psum | solution.py:151
  735.1 5.8 fusion.49
  740.9 4.7 fusion.41
  747.4 10.2 fusion.83
  759.3 39.5 %fusion = (f32[2,5,384]{2,1,0:T(8,128)S(1)}, f32[2,3072,384,5]{2,1,3,0:T(8,128)}) fusion(f32[2,5,384]{2,1,0:T(8,128)S(1)} %copy-done.57, f32[2,5,384]{2,1,0:T(8,128)S(1)} %copy-done.55, f32[2,3072,384,5]{2,1,3,0:T(8,128)} %get-tuple-element.51, pred[384,3072]{0,1:T(8,128)(4,1)S(1)} %copy-done.16, bf16[384,2,5,128]{0,3,2,1:T(8,128)(2,1)S(1)} %bitcast.382, ...), kind=kOutput, calls=%fused_computation.4 | convolution fusion | flops 3090673920 | bytes 98153472 | tf_op jit(solution)/shard_map/bqkgd,bskd->bkgqs/dot_general | solution.py:66
  798.7 23.9 %fusion.192 = (bf16[1,3072,2,128]{1,3,2,0:T(8,128)(2,1)}, f32[1,3072,2,128]{1,3,2,0:T(8,128)}) fusion(bf16[384,2,5,128]{0,3,2,1:T(8,128)(2,1)S(1)} %bitcast.383, f32[2,5,384]{2,1,0:T(8,128)S(1)} %copy-done.57, f32[2,5,384]{2,1,0:T(8,128)S(1)} %copy-done.55, f32[2,3072,384,5]{2,1,3,0:T(8,128)} %get-tuple-element.51, pred[384,3072]{0,1:T(8,128)(4,1)S(1)} %copy-done.16), kind=kOutput, calls=%fused_computation.244 | convolution fusion | flops 3079667712 | bytes 54097920 | tf_op jit(solution)/shard_map/bkgqs,bqkgd->bskd/dot_general | solution.py:65
  822.6 39.2 %fusion.15 = bf16[2,5,384,3072]{2,3,1,0:T(8,128)(2,1)} fusion(f32[2,3072,384,5]{2,1,3,0:T(8,128)} %get-tuple-element.59, f32[2,5,384]{2,1,0:T(8,128)S(1)} %get-tuple-element.58, f32[2,5,384]{2,1,0:T(8,128)S(1)} %copy-done.57, f32[2,5,384]{2,1,0:T(8,128)S(1)} %copy-done.55, f32[2,3072,384,5]{2,1,3,0:T(8,128)} %get-tuple-element.51, ...), kind=kLoop, calls=%fused_computation.23 | loop fusion | flops 94371840 | bytes 119190528 | tf_op jit(solution)/shard_map/reshape.108
  861.8 11.3 fusion.193
  879.9 9.8 fusion.125
  891.5 20.1 fusion.195
  919.2 5.2 collective-permute-done.19
  936.1 8.5 collective-permute-done.25
  949.3 6.8 fusion.55
  956.8 6.4 fusion.168
  963.2 6.3 fusion.166
  970.8 15.2 fusion.179
  987.2 14.3 fusion.68
  1002.7 14.4 fusion.64
  1018.4 15.1 fusion.170
  1039.1 188.7 %all-reduce.16.cloned.1.call-done = (bf16[1,384,5120]{2,1,0:T(8,128)(2,1)}, bf16[1,384,5120]{2,1,0:T(8,128)(2,1)}) async-done(((bf16[1,384,5120]{2,1,0:T(8,128)(2,1)}, bf16[1,384,5120]{2,1,0:T(8,128)(2,1)}), (bf16[1,384,5120]{2,1,0:T(8,128)(2,1)}, bf16[1,384,5120]{2,1,0:T(8,128)(2,1)})) %all-reduce.16.cloned.1.call-update) | async-done | bytes 7864336 | tf_op jit(solution)/shard_map/psum | solution.py:138
  1227.8 4.8 fusion.44
  1232.6 24.7 %all-reduce.6 = (bf16[5120]{0:T(1024)(128)(2,1)S(1)}, bf16[5120]{0:T(1024)(128)(2,1)S(1)}) all-reduce(f32[5120]{0:T(1024)S(1)} %get-tuple-element.14, f32[5120]{0:T(1024)S(1)} %copy-done.58), channel_id=4, replica_groups=mesh['tp'=4,'cp'=8] {'cp'}, use_global_device_ids=true, to_apply=%region_21.22.clone | all-reduce | flops 10240 | bytes 61440
  1258.6 27.8 %reduce-scatter.17.cloned.1.call-done = f32[640,256]{1,0:T(8,128)} async-done(((f32[5120,256]{1,0:T(8,128)}), f32[640,256]{1,0:T(8,128)}) %reduce-scatter.17.cloned.1.call-update) | async-done | bytes 655376 | tf_op jit(solution)/shard_map/reduce_scatter | solution.py:179
  1288.2 58.1 %reduce-scatter.19.cloned.1.call-done = f32[640,256]{1,0:T(8,128)} async-done(((f32[5120,256]{1,0:T(8,128)}), f32[640,256]{1,0:T(8,128)}) %reduce-scatter.19.cloned.1.call-update) | async-done | bytes 655376 | tf_op jit(solution)/shard_map/reduce_scatter | solution.py:179
  1348.2 7.0 fusion.51
  1356.6 4.4 fusion.38
  1361.0 150.0 %reduce-scatter.23.cloned.1.call-done = f32[640,1280]{1,0:T(8,128)} async-done(((f32[5120,1280]{1,0:T(8,128)}), f32[640,1280]{1,0:T(8,128)}) %reduce-scatter.23.cloned.1.call-update) | async-done | bytes 3276816 | tf_op jit(solution)/shard_map/reduce_scatter | solution.py:179
  1514.2 161.5 %reduce-scatter.29.cloned.1.call-done = f32[160,5120]{1,0:T(8,128)} async-done(((f32[1280,5120]{1,0:T(8,128)}), f32[160,5120]{1,0:T(8,128)}) %reduce-scatter.29.cloned.1.call-update) | async-done | bytes 3276816 | tf_op jit(solution)/shard_map/reduce_scatter | solution.py:179
  1679.1 161.1 %reduce-scatter.21.cloned.1.call-done = f32[160,5120]{1,0:T(8,128)} async-done(((f32[1280,5120]{1,0:T(8,128)}), f32[160,5120]{1,0:T(8,128)}) %reduce-scatter.21.cloned.1.call-update) | async-done | bytes 3276816 | tf_op jit(solution)/shard_map/reduce_scatter | solution.py:179
  1843.5 161.3 %reduce-scatter.15.cloned.1.call-done = f32[640,1280]{1,0:T(8,128)} async-done(((f32[5120,1280]{1,0:T(8,128)}), f32[640,1280]{1,0:T(8,128)}) %reduce-scatter.15.cloned.1.call-update) | async-done | bytes 3276816 | tf_op jit(solution)/shard_map/reduce_scatter | solution.py:179
  (302 shorter events, 137.6 us)
Async XLA Ops:
  7.2 322.2 %copy-start = (bf16[5120,256]{1,0:T(8,128)(2,1)S(1)}, bf16[5120,256]{1,0:T(8,128)(2,1)}, u32[]{:S(2)}) copy-start(bf16[5120,256]{1,0:T(8,128)(2,1)} %param.26) | copy-start | bytes 7864324
  7.2 317.0 %all-reduce.12.cloned.1.call-start = ((), (), s32[]{:S(2)}) async-start(), calls=%async_computation.10 | async-start | bytes 7864320 | tf_op jit(solution)/shard_map/psum | solution.py:125
  8.1 31.4 %copy-start.31 = (f32[5120]{0:T(1024)}, f32[5120]{0:T(1024)S(1)}, u32[]{:S(2)}) copy-start(f32[5120]{0:T(1024)S(1)} %convert_element_type.392) | copy-start | bytes 61444
  11.1 28.4 %copy-start.48 = (f32[384]{0:T(512)}, f32[384]{0:T(512)S(1)}, u32[]{:S(2)}) copy-start(f32[384]{0:T(512)S(1)} %add_rsqrt_fusion.1) | copy-start | bytes 4612
  17.4 79.5 %copy-start.12 = (f32[1,384,2,128]{3,1,2,0:T(8,128)}, f32[1,384,2,128]{3,1,2,0:T(8,128)S(1)}, u32[]{:S(2)}) copy-start(f32[1,384,2,128]{3,1,2,0:T(8,128)S(1)} %get-tuple-element.25) | copy-start | bytes 1179652
  17.4 79.4 %copy-start.59 = (f32[384,2]{0,1:T(2,128)}, f32[384,2]{0,1:T(2,128)S(1)}, u32[]{:S(2)}) copy-start(f32[384,2]{0,1:T(2,128)S(1)} %fusion.161) | copy-start | bytes 9220
  18.3 48.8 %collective-permute-start.7 = (bf16[1,384,2,128]{3,1,2,0:T(8,128)(2,1)}, bf16[1,384,2,128]{3,1,2,0:T(8,128)(2,1)}, u32[]{:S(2)}, u32[]{:S(2)}) collective-permute-start(bf16[1,384,2,128]{3,1,2,0:T(8,128)(2,1)} %multiply_convert_fusion.2), channel_id=1, source_target_pairs={{0,7},{8,15},{16,23},{24,31}} | collective-permute-start | bytes 589832 | tf_op jit(solution)/shard_map/ppermute | solution.py:114
  24.4 47.9 %collective-permute-start.8 = (bf16[1,384,2,128]{3,1,2,0:T(8,128)(2,1)}, bf16[1,384,2,128]{3,1,2,0:T(8,128)(2,1)}, u32[]{:S(2)}, u32[]{:S(2)}) collective-permute-start(bf16[1,384,2,128]{3,1,2,0:T(8,128)(2,1)} %multiply_convert_fusion.2), channel_id=1, source_target_pairs={{0,6},{1,7},{8,14},{9,15},{16,22},{17,23},{24,30},{25,31}} | collective-permute-start | bytes 589832 | tf_op jit(solution)/shard_map/ppermute | solution.py:114
  26.3 48.2 %collective-permute-start.9 = (bf16[1,384,2,128]{3,1,2,0:T(8,128)(2,1)}, bf16[1,384,2,128]{3,1,2,0:T(8,128)(2,1)}, u32[]{:S(2)}, u32[]{:S(2)}) collective-permute-start(bf16[1,384,2,128]{3,1,2,0:T(8,128)(2,1)} %multiply_convert_fusion.2), channel_id=1, source_target_pairs={{0,5},{1,6},{2,7},{8,13},{9,14},{10,15},{16,21},{17,22},{18,23},{2... | collective-permute-start | bytes 589832 | tf_op jit(solution)/shard_map/ppermute | solution.py:114
  28.3 48.5 %collective-permute-start.10 = (bf16[1,384,2,128]{3,1,2,0:T(8,128)(2,1)}, bf16[1,384,2,128]{3,1,2,0:T(8,128)(2,1)}, u32[]{:S(2)}, u32[]{:S(2)}) collective-permute-start(bf16[1,384,2,128]{3,1,2,0:T(8,128)(2,1)} %multiply_convert_fusion.2), channel_id=1, source_target_pairs={{0,4},{1,5},{2,6},{3,7},{8,12},{9,13},{10,14},{11,15},{16,20},{17,... | collective-permute-start | bytes 589832 | tf_op jit(solution)/shard_map/ppermute | solution.py:114
  35.6 33.7 %collective-permute-start = (bf16[1,384,2,128]{1,3,2,0:T(8,128)(2,1)}, bf16[1,384,2,128]{1,3,2,0:T(8,128)(2,1)}, u32[]{:S(2)}, u32[]{:S(2)}) collective-permute-start(bf16[1,384,2,128]{1,3,2,0:T(8,128)(2,1)} %bitcast.1), channel_id=1, source_target_pairs={{0,7},{8,15},{16,23},{24,31}} | collective-permute-start | bytes 589832 | tf_op jit(solution)/shard_map/ppermute | solution.py:115
  37.7 25.8 %copy-start.24 = (f32[384,128]{0,1:T(8,128)}, f32[384,128]{0,1:T(8,128)S(1)}, u32[]{:S(2)}) copy-start(f32[384,128]{0,1:T(8,128)S(1)} %copy.96) | copy-start | bytes 589828
  38.9 24.6 %copy-start.26 = (f32[384,128]{0,1:T(8,128)}, f32[384,128]{0,1:T(8,128)S(1)}, u32[]{:S(2)}) copy-start(f32[384,128]{0,1:T(8,128)S(1)} %copy.98) | copy-start | bytes 589828
  58.6 30.4 %copy-start.44 = (f32[384,10]{0,1:T(8,128)}, f32[384,10]{0,1:T(8,128)S(1)}, u32[]{:S(2)}) copy-start(f32[384,10]{0,1:T(8,128)S(1)} %fusion.147) | copy-start | bytes 46084
  67.1 12.0 collective-permute-start.11
  69.3 13.3 collective-permute-start.12
  72.2 11.7 collective-permute-start.13
  74.5 10.8 collective-permute-start.1
  76.8 11.5 collective-permute-start.2
  79.1 15.7 collective-permute-start.3
  82.6 12.8 collective-permute-start.4
  84.0 12.2 collective-permute-start.5
  85.3 12.9 collective-permute-start.6
  141.5 21.3 %copy-start.56 = (f32[2,5,384]{2,1,0:T(8,128)}, f32[2,5,384]{2,1,0:T(8,128)S(1)}, u32[]{:S(2)}) copy-start(f32[2,5,384]{2,1,0:T(8,128)S(1)} %fusion.9) | copy-start | bytes 46084
  175.5 181.3 %all-gather.5.cloned.1.call-start = ((), (), s32[]{:S(2)}) async-start(), calls=%async_computation.12 | async-start | bytes 1769472 | tf_op jit(solution)/shard_map/all_gather | solution.py:133
  176.0 174.7 %copy-start.33 = (f32[5120]{0:T(1024)}, f32[5120]{0:T(1024)S(1)}, u32[]{:S(2)}) copy-start(f32[5120]{0:T(1024)S(1)} %convert_element_type.414) | copy-start | bytes 61444
  176.0 160.3 %copy-start.63 = (f32[384]{0:T(512)}, f32[384]{0:T(512)S(1)}, u32[]{:S(2)}) copy-start(f32[384]{0:T(512)S(1)} %fusion.158) | copy-start | bytes 4612
  332.1 65.1 %all-gather.3.cloned.1.call-start = ((), (), s32[]{:S(2)}) async-start(), calls=%async_computation.11 | async-start | bytes 1769472 | tf_op jit(solution)/shard_map/all_gather | solution.py:134
  356.0 199.3 %reduce-scatter.31.cloned.1.call-start = ((), (), s32[]{:S(2)}) async-start(), calls=%async_computation.22 | async-start | bytes 1769472
  397.1 36.5 %copy-start.17 = (pred[384,3072]{0,1:T(8,128)(4,1)S(1)}, pred[384,3072]{0,1:T(8,128)(4,1)}, u32[]{:S(2)}) copy-start(pred[384,3072]{0,1:T(8,128)(4,1)} %iota_compare_fusion) | copy-start | bytes 3538948
  493.1 21.9 %copy-start.64 = (f32[384]{0:T(512)S(1)}, f32[384]{0:T(512)}, u32[]{:S(2)}) copy-start(f32[384]{0:T(512)} %copy-done.63) | copy-start | bytes 4612
  493.2 84.4 %reduce-scatter.33.cloned.1.call-start = ((), (), s32[]{:S(2)}) async-start(), calls=%async_computation.23 | async-start | bytes 1769472
  539.1 196.0 %all-reduce.14.cloned.1.call-start = ((), (), s32[]{:S(2)}) async-start(), calls=%async_computation.13 | async-start | bytes 7864320 | tf_op jit(solution)/shard_map/psum | solution.py:151
  588.4 447.0 %reduce-scatter.25.cloned.1.call-start = ((), (), s32[]{:S(2)}) async-start(), calls=%async_computation.19 | async-start | bytes 5898240 | tf_op jit(solution)/shard_map/reduce_scatter | solution.py:179
  595.0 442.2 %reduce-scatter.27.cloned.1.call-start = ((), (), s32[]{:S(2)}) async-start(), calls=%async_computation.20 | async-start | bytes 5898240 | tf_op jit(solution)/shard_map/reduce_scatter | solution.py:179
  633.6 594.1 %all-reduce.16.cloned.1.call-start = ((), (), s32[]{:S(2)}) async-start(), calls=%async_computation.24 | async-start | bytes 15728640 | tf_op jit(solution)/shard_map/psum | solution.py:138
  822.6 39.2 %copy-start.14 = (bf16[384,2,5,128]{0,3,2,1:T(8,128)(2,1)S(1)}, bf16[384,2,5,128]{0,3,2,1:T(8,128)(2,1)}, u32[]{:S(2)}) copy-start(bf16[384,2,5,128]{0,3,2,1:T(8,128)(2,1)} %fusion.92) | copy-start | bytes 2949124
  873.2 38.4 %collective-permute-start.14 = (bf16[1,384,2,128]{3,1,2,0:T(8,128)(2,1)S(1)}, bf16[1,384,2,128]{3,1,2,0:T(8,128)(2,1)S(1)}, u32[]{:S(2)}, u32[]{:S(2)}) collective-permute-start(bf16[1,384,2,128]{3,1,2,0:T(8,128)(2,1)S(1)} %get-tuple-element.32), channel_id=1, source_target_pairs={{1,0},{2,1},{3,2},{4,3},{5,4},{6,5},{7,6},{9,8},{10,9},{11,10},{12... | collective-permute-start | bytes 589832 | tf_op jit(solution)/shard_map/ppermute | solution.py:165
  874.5 38.6 %collective-permute-start.15 = (bf16[1,384,2,128]{3,1,2,0:T(8,128)(2,1)S(1)}, bf16[1,384,2,128]{3,1,2,0:T(8,128)(2,1)S(1)}, u32[]{:S(2)}, u32[]{:S(2)}) collective-permute-start(bf16[1,384,2,128]{3,1,2,0:T(8,128)(2,1)S(1)} %get-tuple-element.38), channel_id=1, source_target_pairs={{2,0},{3,1},{4,2},{5,3},{6,4},{7,5},{10,8},{11,9},{12,10},{13,11},... | collective-permute-start | bytes 589832 | tf_op jit(solution)/shard_map/ppermute | solution.py:165
  875.8 39.5 %collective-permute-start.16 = (bf16[1,384,2,128]{3,1,2,0:T(8,128)(2,1)S(1)}, bf16[1,384,2,128]{3,1,2,0:T(8,128)(2,1)S(1)}, u32[]{:S(2)}, u32[]{:S(2)}) collective-permute-start(bf16[1,384,2,128]{3,1,2,0:T(8,128)(2,1)S(1)} %get-tuple-element.37), channel_id=1, source_target_pairs={{3,0},{4,1},{5,2},{6,3},{7,4},{11,8},{12,9},{13,10},{14,11},{15,12... | collective-permute-start | bytes 589832 | tf_op jit(solution)/shard_map/ppermute | solution.py:165
  877.1 39.5 %collective-permute-start.17 = (bf16[1,384,2,128]{3,1,2,0:T(8,128)(2,1)S(1)}, bf16[1,384,2,128]{3,1,2,0:T(8,128)(2,1)S(1)}, u32[]{:S(2)}, u32[]{:S(2)}) collective-permute-start(bf16[1,384,2,128]{3,1,2,0:T(8,128)(2,1)S(1)} %get-tuple-element.36), channel_id=1, source_target_pairs={{4,0},{5,1},{6,2},{7,3},{12,8},{13,9},{14,10},{15,11},{20,16},{21,... | collective-permute-start | bytes 589832 | tf_op jit(solution)/shard_map/ppermute | solution.py:165
  878.4 39.5 %collective-permute-start.18 = (bf16[1,384,2,128]{3,1,2,0:T(8,128)(2,1)S(1)}, bf16[1,384,2,128]{3,1,2,0:T(8,128)(2,1)S(1)}, u32[]{:S(2)}, u32[]{:S(2)}) collective-permute-start(bf16[1,384,2,128]{3,1,2,0:T(8,128)(2,1)S(1)} %get-tuple-element.35), channel_id=1, source_target_pairs={{5,0},{6,1},{7,2},{13,8},{14,9},{15,10},{21,16},{22,17},{23,18},{2... | collective-permute-start | bytes 589832 | tf_op jit(solution)/shard_map/ppermute | solution.py:165
  891.5 22.9 %copy-start.43 = (bf16[1,3072,2,128]{1,3,2,0:T(8,128)(2,1)S(1)}, bf16[1,3072,2,128]{1,3,2,0:T(8,128)(2,1)}, u32[]{:S(2)}) copy-start(bf16[1,3072,2,128]{1,3,2,0:T(8,128)(2,1)} %get-tuple-element.56) | copy-start | bytes 4718596
  891.5 38.7 %copy-start.13 = (f32[1,384,2,128]{3,1,2,0:T(8,128)S(1)}, f32[1,384,2,128]{3,1,2,0:T(8,128)}, u32[]{:S(2)}) copy-start(f32[1,384,2,128]{3,1,2,0:T(8,128)} %copy-done.12) | copy-start | bytes 1179652
  891.5 39.0 %copy-start.62 = (f32[384,2]{0,1:T(2,128)S(1)}, f32[384,2]{0,1:T(2,128)}, u32[]{:S(2)}) copy-start(f32[384,2]{0,1:T(2,128)} %copy-done.61) | copy-start | bytes 9220
  891.5 39.0 %copy-start.60 = (f32[384,2]{0,1:T(2,128)S(1)}, f32[384,2]{0,1:T(2,128)}, u32[]{:S(2)}) copy-start(f32[384,2]{0,1:T(2,128)} %copy-done.59) | copy-start | bytes 9220
  911.6 22.0 %copy-start.38 = (f32[384,128]{1,0:T(8,128)S(1)}, f32[384,128]{1,0:T(8,128)}, u32[]{:S(2)}) copy-start(f32[384,128]{1,0:T(8,128)} %param.17) | copy-start | bytes 589828
  911.6 12.9 collective-permute-start.19
  913.0 15.8 collective-permute-start.20
  915.3 15.6 collective-permute-start.21
  916.6 15.7 collective-permute-start.22
  917.9 16.2 collective-permute-start.23
  924.5 11.6 collective-permute-start.24
  928.9 15.7 collective-permute-start.25
  931.0 13.6 collective-permute-start.26
  932.3 12.3 collective-permute-start.27
  956.1 330.3 %reduce-scatter.17.cloned.1.call-start = ((), (), s32[]{:S(2)}) async-start(), calls=%async_computation.15 | async-start | bytes 5898240 | tf_op jit(solution)/shard_map/reduce_scatter | solution.py:179
  963.2 383.1 %reduce-scatter.19.cloned.1.call-start = ((), (), s32[]{:S(2)}) async-start(), calls=%async_computation.16 | async-start | bytes 5898240 | tf_op jit(solution)/shard_map/reduce_scatter | solution.py:179
  969.6 541.3 %reduce-scatter.23.cloned.1.call-start = ((), (), s32[]{:S(2)}) async-start(), calls=%async_computation.18 | async-start | bytes 29491200 | tf_op jit(solution)/shard_map/reduce_scatter | solution.py:179
  986.0 689.6 %reduce-scatter.29.cloned.1.call-start = ((), (), s32[]{:S(2)}) async-start(), calls=%async_computation.21 | async-start | bytes 29491200 | tf_op jit(solution)/shard_map/reduce_scatter | solution.py:179
  1001.6 838.7 %reduce-scatter.21.cloned.1.call-start = ((), (), s32[]{:S(2)}) async-start(), calls=%async_computation.17 | async-start | bytes 29491200 | tf_op jit(solution)/shard_map/reduce_scatter | solution.py:179
  1017.2 987.7 %reduce-scatter.15.cloned.1.call-start = ((), (), s32[]{:S(2)}) async-start(), calls=%async_computation.14 | async-start | bytes 29491200 | tf_op jit(solution)/shard_map/reduce_scatter | solution.py:179
  1033.5 199.1 %copy-start.58 = (f32[5120]{0:T(1024)S(1)}, f32[5120]{0:T(1024)}, u32[]{:S(2)}) copy-start(f32[5120]{0:T(1024)} %get-tuple-element.12) | copy-start | bytes 61444
  1675.7 332.4 %copy-start.1 = (bf16[5120,256]{1,0:T(8,128)(2,1)S(1)}, bf16[5120,256]{1,0:T(8,128)(2,1)}, u32[]{:S(2)}) copy-start(bf16[5120,256]{1,0:T(8,128)(2,1)} %param.26) | copy-start | bytes 7864324
  (47 other events, 377.6 us)
Sparse Core Ops, SparseCore 0:
  175.6 148.5 all-reduce.11
  332.2 24.5 all-gather.4
  359.2 25.7 all-gather.2
  493.3 38.3 reduce-scatter.30
  539.2 38.3 reduce-scatter.32
  588.5 146.4 all-reduce.13
  738.5 55.5 reduce-scatter.24
  797.4 56.5 reduce-scatter.26
  956.2 271.4 all-reduce.15
  1231.0 55.3 reduce-scatter.16
  1289.8 56.5 reduce-scatter.18
  1349.9 161.0 reduce-scatter.22
  1514.6 161.0 reduce-scatter.28
  1679.2 161.0 reduce-scatter.20
  1843.8 161.0 reduce-scatter.14
where the time goes:
time: 2030 us; the launch traced here: 2020 us
  waiting for transfers between devices  1190 us (59%)
  matrix products  486 us (24%)
  other arithmetic  194 us (10%)
  local copies, waits for them, and re-layouts  60.4 us (3%)
  starting transfers between devices  48.8 us (2%)
  blocking collectives  24.7 us (1%)
    reduce_scatter x8, waiting for transfers between devices, to_rows(): lax.psum_scatter(part, 'cp', scatter_dimension=0, tiled=True)  720 us
    psum x1, waiting for transfers between devices, body(): attn_b = lax.psum(project(out_b, wo_b), 'tp')  189 us
    psum x1, waiting for transfers between devices, body(): attn_a = lax.psum(project(out_a, wo_a), 'tp')  133 us
    psum x1, waiting for transfers between devices, body(): grad_xn_b = lax.psum(grad_xn_b.astype(jnp.bfloat16), 'tp')  101 us
    dot_general x8, matrix products, project_back(): jnp.einsum('bsh,dh->bsd', grad_out, weight, preferred_element_type=jnp.fl...  85.4 us
    dot_general x8, matrix products, weight_grad(): jnp.einsum('bsd,bsh->dh', act, grad_out, preferred_element_type=jnp.float32)  82.6 us
    another operation x2, other arithmetic  77.5 us
    dot_general x2, matrix products, attn_backward(): jnp.einsum('bqkgd,bskd->bkgqs', grad_out, values, preferred_element_type=...  76 us
  transfers between devices with their start and end apart: 43, of which 16 were waited for; matrix products, arithmetic and copies ran while one was open for 26% of the time, Pallas kernels for 0%

commit v1 on v0

v1 whole, which is shorter than its diff:
```python
import functools
import jax
import jax.numpy as jnp
from jax import lax
from jax.experimental import pallas as pl
from jax.experimental.pallas import tpu as pltpu
from jax.sharding import PartitionSpec as P

CHUNK = 8192
NORM_EPS = 1e-5
QK_EPS = 1e-6
TEMP_SCALE = 0.1
NEG_BIG = -1e30
JOIN = 8
LOG2E = 1.4426950408889634


def rms_norm(act, gamma):
    act_wide = act.astype(jnp.float32)
    inv_rms = lax.rsqrt(jnp.mean(act_wide * act_wide, axis=-1, keepdims=True) + NORM_EPS)
    return (act_wide * inv_rms * gamma.astype(jnp.float32)).astype(jnp.bfloat16)


def norm_backward(act, gamma, grad_out):
    act_wide = act.astype(jnp.float32)
    inv_rms = lax.rsqrt(jnp.mean(act_wide * act_wide, axis=-1, keepdims=True) + NORM_EPS)
    x_hat = act_wide * inv_rms
    grad_hat = grad_out * gamma.astype(jnp.float32)
    return inv_rms * (grad_hat - x_hat * jnp.mean(grad_hat * x_hat, axis=-1, keepdims=True))


def rotate(wide, cos_tab, sin_tab):
    half = wide.shape[-1] // 2
    turned = jnp.concatenate([-wide[..., half:], wide[..., :half]], axis=-1)
    return wide * cos_tab[:, None, :] + turned * sin_tab[:, None, :]


def qk_prep(raw_val, cos_tab, sin_tab):
    wide = rotate(raw_val.astype(jnp.float32), cos_tab, sin_tab)
    return (wide * lax.rsqrt(jnp.mean(wide * wide, axis=-1, keepdims=True) + QK_EPS)).astype(jnp.bfloat16)


def temperature(positions):
    return jnp.log(((positions + 1) // CHUNK).astype(jnp.float32) + 1.0) * TEMP_SCALE + 1.0


def dot(lhs, rhs, lhs_dim, rhs_dim):
    return lax.dot_general(lhs, rhs, (((lhs_dim,), (rhs_dim,)), ((), ())), preferred_element_type=jnp.float32)


def masked_scores(raw, first_key, first_query, cut):
    key_at = first_key + lax.broadcasted_iota(jnp.int32, raw.shape, 0)
    query_at = first_query + lax.broadcasted_iota(jnp.int32, (1, raw.shape[1]), 1)
    lowest = jnp.where(query_at >= cut, cut, 0)
    return jnp.where((key_at <= query_at) & (key_at >= lowest), raw, NEG_BIG)


def attn_fwd_kernel(local, coef, info, q_ref, k_ref, v_ref, o_ref, lse_ref, score):
    rank, cut = info[0], info[1]
    block, width = q_ref.shape
    queries = q_ref[...]
    span = score.shape[2]
    n_lane = span // width
    last = rank // (span // block)

    def rows(step):
        return pl.ds(pl.multiple_of(step * span, span), span)

    def raw_step(step, carry, masked):
        top, total = carry
        raw = dot(queries, k_ref[rows(step), :], 1, 1)
        if masked:
            query_at = rank * block + lax.broadcasted_iota(jnp.int32, (block, 1), 0)
            key_at = step * span + lax.broadcasted_iota(jnp.int32, raw.shape, 1)
            lowest = jnp.where(query_at >= cut, cut, 0)
            raw = jnp.where((key_at <= query_at) & (key_at >= lowest), raw, NEG_BIG)
        score[step] = raw
        parts = [raw[:, at * width:(at + 1) * width] * coef for at in range(n_lane)]
        higher = functools.reduce(jnp.maximum, parts, top)
        total = total * jnp.exp2(top - higher)
        for part in parts:
            total += jnp.exp2(part - higher)
        return higher, total

    carry = (jnp.full((block, width), NEG_BIG, jnp.float32), jnp.zeros((block, width), jnp.float32))
    carry = lax.fori_loop(0, last, lambda s, c: raw_step(s, c, local), carry)
    lane_top, lane_total = raw_step(last, carry, True)
    top = jnp.max(lane_top, axis=1, keepdims=True)
    total = jnp.sum(lane_total * jnp.exp2(lane_top - top), axis=1, keepdims=True)
    lse = top + jnp.log2(total)

    def out_step(step, acc):
        prob = jnp.exp2(score[step] * coef - lse).astype(jnp.bfloat16)
        return acc + dot(prob, v_ref[rows(step), :], 1, 0)

    acc = lax.fori_loop(0, last + 1, out_step, jnp.zeros((block, width), jnp.float32))
    o_ref[...] = acc.astype(jnp.bfloat16)
    lse_ref[0] = jnp.broadcast_to(lse, (block, width)).T[:1]


def attn_bwd_kernel(local, coef, scale, groups, info, q_ref, k_ref, v_ref, o_ref, do_ref, lse_ref,
                    dq_ref, dkv_ref, dk_acc, dv_acc):
    head = pl.program_id(0)
    group = lax.rem(head, groups)
    rank, cut = info[0], info[1]
    block, width = q_ref.shape
    span = JOIN * block
    last = rank // JOIN
    queries = q_ref[...]
    grads = do_ref[...]
    lse = lse_ref[0]
    delta = jnp.sum((grads.astype(jnp.float32) * o_ref[...].astype(jnp.float32)).T, axis=0, keepdims=True)

    @pl.when(group == 0)
    def _():
        dk_acc[...] = jnp.zeros_like(dk_acc)
        dv_acc[...] = jnp.zeros_like(dv_acc)

    def step_fn(step, acc, masked):
        where = pl.ds(pl.multiple_of(step * span, span), span)
        keys = k_ref[where, :]
        raw = dot(keys, queries, 1, 1)
        if masked:
            raw = masked_scores(raw, step * span, rank * block, cut)
        prob = jnp.exp2(raw * coef - lse)
        dprob = dot(v_ref[where, :], grads, 1, 1)
        dscore = (prob * (dprob - delta) * scale).astype(jnp.bfloat16)
        dv_acc[where, :] += dot(prob.astype(jnp.bfloat16), grads, 1, 0)
        dk_acc[where, :] += dot(dscore, queries, 1, 0)
        return acc + dot(keys, dscore, 0, 0)

    acc = lax.fori_loop(0, last, lambda s, a: step_fn(s, a, local), jnp.zeros((width, block), jnp.float32))
    acc = step_fn(last, acc, True)
    dq_ref[...] = acc.T.astype(dq_ref.dtype)
    kv_local = dkv_ref.shape[1] // (2 * width)
    for kv in range(kv_local):
        @pl.when(head == kv * groups + groups - 1)
        def _():
            dkv_ref[:, kv * width:(kv + 1) * width] = dk_acc[...].astype(jnp.bfloat16)
            dkv_ref[:, (kv_local + kv) * width:(kv_local + kv + 1) * width] = dv_acc[...].astype(jnp.bfloat16)


def attn_specs(seq_len, block, width, kv_local, groups):
    return [pl.BlockSpec((block, width), lambda h, info: (0, h)),
            pl.BlockSpec((seq_len, width), lambda h, info: (0, h // groups)),
            pl.BlockSpec((seq_len, width), lambda h, info: (0, kv_local + h // groups))]


def attn_forward(local, info, query, kv_all, width):
    block, seq_len = query.shape[0], kv_all.shape[0]
    heads, kv_local = query.shape[1] // width, kv_all.shape[1] // (2 * width)
    groups = heads // kv_local
    scale = width ** -0.5
    flops = 4 * heads * block * seq_len * width
    return pl.pallas_call(
        functools.partial(attn_fwd_kernel, local, scale * LOG2E),
        out_shape=(jax.ShapeDtypeStruct(query.shape, jnp.bfloat16), jax.ShapeDtypeStruct((heads, 1, block), jnp.float32)),
        grid_spec=pltpu.PrefetchScalarGridSpec(
            num_scalar_prefetch=1, grid=(heads,),
            in_specs=attn_specs(seq_len, block, width, kv_local, groups),
            out_specs=[pl.BlockSpec((block, width), lambda h, info: (0, h)),
                       pl.BlockSpec((1, 1, block), lambda h, info: (h, 0, 0))],
            scratch_shapes=[pltpu.VMEM((seq_len // (JOIN * block), block, JOIN * block), jnp.float32)]),
        compiler_params=pltpu.CompilerParams(vmem_limit_bytes=40 * 2 ** 20),
        cost_estimate=pl.CostEstimate(flops=flops * 4, bytes_accessed=8 * 2 ** 20, transcendentals=0),
        name='attn_fwd_a' if local else 'attn_fwd_b',
    )(info, query, kv_all, kv_all)


def attn_backward(local, info, query, kv_all, out, grad_out, lse, width, dq_dtype):
    block, seq_len = query.shape[0], kv_all.shape[0]
    heads, kv_local = query.shape[1] // width, kv_all.shape[1] // (2 * width)
    groups = heads // kv_local
    scale = width ** -0.5
    flops = 10 * heads * block * seq_len * width
    head_spec = pl.BlockSpec((block, width), lambda h, info: (0, h))
    return pl.pallas_call(
        functools.partial(attn_bwd_kernel, local, scale * LOG2E, scale, groups),
        out_shape=(jax.ShapeDtypeStruct(query.shape, dq_dtype), jax.ShapeDtypeStruct(kv_all.shape, jnp.bfloat16)),
        grid_spec=pltpu.PrefetchScalarGridSpec(
            num_scalar_prefetch=1, grid=(heads,),
            in_specs=attn_specs(seq_len, block, width, kv_local, groups)
            + [head_spec, head_spec, pl.BlockSpec((1, 1, block), lambda h, info: (h, 0, 0))],
            out_specs=[head_spec, pl.BlockSpec(kv_all.shape, lambda h, info: (0, 0))],
            scratch_shapes=[pltpu.VMEM((seq_len, width), jnp.float32), pltpu.VMEM((seq_len, width), jnp.float32)]),
        compiler_params=pltpu.CompilerParams(vmem_limit_bytes=40 * 2 ** 20),
        cost_estimate=pl.CostEstimate(flops=flops * 4, bytes_accessed=12 * 2 ** 20, transcendentals=0),
        name='attn_bwd_a' if local else 'attn_bwd_b',
    )(info, query, kv_all, kv_all, out, grad_out, lse)


def wgrad_kernel(n_blocks, flip, *refs):
    acts, grads = refs[:n_blocks], refs[n_blocks:2 * n_blocks]
    out_ref, turned = refs[2 * n_blocks], refs[2 * n_blocks + 1]
    block = acts[0].shape[0]

    @pl.when(pl.program_id(0) == 0)
    def _():
        for at, act in enumerate(acts):
            turned[:, at * block:(at + 1) * block] = act[...].T

    acc = dot(turned[:, :block], grads[0][...], 1, 0)
    for at in range(1, n_blocks):
        acc += dot(turned[:, at * block:(at + 1) * block], grads[at][...], 1, 0)
    out_ref[...] = (acc.T if flip else acc).astype(jnp.bfloat16)


def weight_grad(acts, grads, flip=False):
    n_blocks = len(acts)
    block, rows = acts[0].shape
    cols = grads[0].shape[1]
    tile = 256
    return pl.pallas_call(
        functools.partial(wgrad_kernel, n_blocks, flip),
        out_shape=jax.ShapeDtypeStruct((cols, rows) if flip else (rows, cols), jnp.bfloat16),
        grid=(cols // tile,),
        in_specs=[pl.BlockSpec((block, rows), lambda j: (0, 0))] * n_blocks
        + [pl.BlockSpec((block, tile), lambda j: (0, j))] * n_blocks,
        out_specs=pl.BlockSpec((tile, rows), lambda j: (j, 0)) if flip else pl.BlockSpec((rows, tile), lambda j: (0, j)),
        scratch_shapes=[pltpu.VMEM((rows, n_blocks * block), jnp.bfloat16)],
        compiler_params=pltpu.CompilerParams(vmem_limit_bytes=48 * 2 ** 20),
        cost_estimate=pl.CostEstimate(flops=2 * n_blocks * block * rows * cols, bytes_accessed=16 * 2 ** 20, transcendentals=0),
    )(*acts, *grads)


def solution(mesh):
    cp_size = mesh.shape['cp']
    row_spec = P(None, 'cp', None)
    col_spec = P(None, 'tp')
    grid_spec = P('cp', 'tp')
    out_rows = P(('tp', 'cp'), None)
    in_specs = (row_spec, P('cp'), P('cp', None), P('cp', None),
                P(None), col_spec, col_spec, col_spec, P('tp', None),
                P(None), col_spec, col_spec, col_spec, P('tp', None), row_spec)
    out_specs = (row_spec, row_spec,
                 P('cp'), grid_spec, grid_spec, grid_spec, out_rows,
                 P('cp'), grid_spec, grid_spec, grid_spec, out_rows)

    def swap(val, mask):
        return lax.ppermute(val, 'cp', [(source, source ^ mask) for source in range(cp_size)])

    def gather_xor(val):
        near = [val] + [swap(val, mask) for mask in range(2, cp_size, 2)]
        return near + [swap(part, 1) for part in near]

    order = list(range(0, cp_size, 2)) + [mask ^ 1 for mask in range(0, cp_size, 2)]

    def exchange_cols(val):
        cols = val.shape[1] // cp_size
        rank = lax.axis_index('cp')
        return [(lambda piece: piece if mask == 0 else swap(piece, mask))(
            lax.dynamic_slice_in_dim(val, (rank ^ mask) * cols, cols, axis=1)) for mask in order]

    def gain_grad(act, partial):
        act_wide = act.astype(jnp.float32)
        inv_rms = lax.rsqrt(jnp.mean(act_wide * act_wide, axis=-1, keepdims=True) + NORM_EPS)
        total = jnp.sum(partial.astype(jnp.float32) * (act_wide * inv_rms), axis=0)
        rank = lax.axis_index('cp')
        mask = cp_size // 2
        while mask:
            rows = total.shape[0] // 2
            upper = (rank // mask) % 2
            theirs = swap(lax.dynamic_slice_in_dim(total, (1 - upper) * rows, rows), mask)
            total = lax.dynamic_slice_in_dim(total, upper * rows, rows) + theirs
            mask //= 2
        mask = 1
        while mask < mesh.shape['tp']:
            total = total + lax.ppermute(total, 'tp', [(source, source ^ mask) for source in range(mesh.shape['tp'])])
            mask *= 2
        return total.astype(jnp.bfloat16)

    def exchange_rows(val):
        return lax.all_to_all(val, 'cp', split_axis=0, concat_axis=1, tiled=True)

    def body(x_in, positions, rope_cos, rope_sin, norm_a, wq_a, wk_a, wv_a, wo_a,
             norm_b, wq_b, wk_b, wv_b, wo_b, grad_y):
        x_in, grad_y = x_in[0], grad_y[0]
        block = x_in.shape[0]
        width = rope_cos.shape[1]
        kv_local = wk_a.shape[1] // width
        kv_cols = kv_local * width
        cp_rank = lax.axis_index('cp')
        first = positions[0] - cp_rank * block
        info_a = jnp.stack([cp_rank, lax.rem(CHUNK - lax.rem(first, CHUNK), CHUNK)]).astype(jnp.int32)
        info_b = jnp.stack([cp_rank, jnp.zeros_like(cp_rank)]).astype(jnp.int32)
        q_temp = temperature(positions)[:, None]

        def prep(raw_val):
            heads = raw_val.reshape(block, -1, width)
            return qk_prep(heads, rope_cos, rope_sin).reshape(raw_val.shape)

        def project(act, weight):
            return dot(act, weight, 1, 0).astype(jnp.bfloat16)

        def gather_kv(key, value):
            return lax.all_gather(jnp.concatenate([key, value], axis=1), 'cp', axis=0, tiled=True)

        def scatter_kv(grad):
            return lax.psum_scatter(grad, 'cp', scatter_dimension=0, tiled=True)

        grad_y_cols = exchange_cols(grad_y)
        xn_a = rms_norm(x_in, norm_a)
        key_a, k_pull = jax.vjp(prep, project(xn_a, wk_a))
        kv_a = gather_kv(key_a, project(xn_a, wv_a))
        query_a, q_pull = jax.vjp(prep, project(xn_a, wq_a))
        xn_a_cols = exchange_cols(xn_a)
        out_a, lse_a = attn_forward(True, info_a, query_a, kv_a, width)
        attn_a = lax.psum(project(out_a, wo_a), 'tp')
        out_a_all = gather_xor(out_a)
        grad_ob = dot(grad_y, wo_b, 1, 1).astype(jnp.bfloat16)
        attn_a, grad_ob, grad_y_cols, xn_a_cols, out_a_all = lax.optimization_barrier(
            (attn_a, grad_ob, grad_y_cols, xn_a_cols, out_a_all))
        h_mid = (x_in.astype(jnp.float32) + attn_a.astype(jnp.float32)).astype(jnp.bfloat16)

        xn_b = rms_norm(h_mid, norm_b)
        kv_b = gather_kv(project(xn_b, wk_b), project(xn_b, wv_b))
        query_b = (project(xn_b, wq_b).astype(jnp.float32) * q_temp).astype(jnp.bfloat16)
        kv_b, xn_b_late = lax.optimization_barrier((kv_b, xn_b))
        xn_b_cols = exchange_cols(xn_b_late)
        out_b, lse_b = attn_forward(False, info_b, query_b, kv_b, width)
        attn_b = project(out_b, wo_b)
        attn_b, lse_b, xn_b_cols = lax.optimization_barrier((attn_b, lse_b, xn_b_cols))
        half = block // 2
        attn_b_lo = lax.psum(attn_b[:half], 'tp')
        out_b_all = gather_xor(out_b)

        grad_q_b, grad_kv_b = attn_backward(False, info_b, query_b, kv_b, out_b, grad_ob, lse_b, width, jnp.float32)
        grad_kv_b, attn_b_lo = lax.optimization_barrier((grad_kv_b, attn_b_lo))
        grad_kv_b = scatter_kv(grad_kv_b)
        grad_q_b = (grad_q_b * q_temp).astype(jnp.bfloat16)
        grad_q_b_all, grad_kv_b_all = gather_xor(grad_q_b), gather_xor(grad_kv_b)
        grad_xn_b = dot(grad_q_b, wq_b, 1, 1) + dot(grad_kv_b[:, :kv_cols], wk_b, 1, 1) + dot(grad_kv_b[:, kv_cols:], wv_b, 1, 1)
        grad_xn_b = grad_xn_b.astype(jnp.bfloat16)
        grad_norm_b = gain_grad(h_mid, grad_xn_b)
        grad_xn_b = lax.psum(grad_xn_b, 'tp')
        grad_wo_b = weight_grad(grad_y_cols, out_b_all, True)
        grad_wq_b = weight_grad(xn_b_cols, grad_q_b_all)
        grad_wkv_b = weight_grad(xn_b_cols, grad_kv_b_all)
        grad_xn_b, grad_wo_b, grad_wq_b, grad_wkv_b, grad_norm_b, attn_b = lax.optimization_barrier(
            (grad_xn_b, grad_wo_b, grad_wq_b, grad_wkv_b, grad_norm_b, attn_b))
        attn_b_hi = lax.psum(attn_b[half:], 'tp')
        grad_h = (grad_y.astype(jnp.float32) + norm_backward(h_mid, norm_b, grad_xn_b.astype(jnp.float32))).astype(jnp.bfloat16)

        grad_h_cols = exchange_cols(grad_h)
        grad_oa = dot(grad_h, wo_a, 1, 1).astype(jnp.bfloat16)
        grad_q_a, grad_kv_a = attn_backward(True, info_a, query_a, kv_a, out_a, grad_oa, lse_a, width, jnp.bfloat16)
        grad_kv_a, attn_b_hi, grad_h_cols = lax.optimization_barrier((grad_kv_a, attn_b_hi, grad_h_cols))
        attn_b = jnp.concatenate([attn_b_lo, attn_b_hi], axis=0)
        out_y = (h_mid.astype(jnp.float32) + attn_b.astype(jnp.float32)).astype(jnp.bfloat16)
        grad_kv_a = scatter_kv(grad_kv_a)
        grad_q_a = q_pull(grad_q_a)[0]
        grad_kv_a, grad_q_a_late, grad_wo_b = lax.optimization_barrier((grad_kv_a, grad_q_a, grad_wo_b))
        grad_q_a_all = gather_xor(grad_q_a_late)
        grad_wo_b = exchange_rows(grad_wo_b)
        grad_k_a = k_pull(grad_kv_a[:, :kv_cols])[0]
        grad_v_a = grad_kv_a[:, kv_cols:]
        grad_kv_a_all = gather_xor(jnp.concatenate([grad_k_a, grad_v_a], axis=1))
        grad_xn_a = dot(grad_q_a, wq_a, 1, 1) + dot(grad_k_a, wk_a, 1, 1) + dot(grad_v_a, wv_a, 1, 1)
        grad_xn_a = grad_xn_a.astype(jnp.bfloat16)
        grad_norm_a = gain_grad(x_in, grad_xn_a)
        grad_xn_a = lax.psum(grad_xn_a, 'tp')
        grad_wo_a = exchange_rows(weight_grad(grad_h_cols, out_a_all, True))
        grad_wq_a = weight_grad(xn_a_cols, grad_q_a_all)
        grad_wkv_a = weight_grad(xn_a_cols, grad_kv_a_all)
        grad_xn_a, grad_wo_a, grad_wq_a, grad_wkv_a, grad_norm_a, grad_wo_b, out_y = lax.optimization_barrier(
            (grad_xn_a, grad_wo_a, grad_wq_a, grad_wkv_a, grad_norm_a, grad_wo_b, out_y))
        grad_x = (grad_h.astype(jnp.float32) + norm_backward(x_in, norm_a, grad_xn_a.astype(jnp.float32))).astype(jnp.bfloat16)

        return (out_y[None], grad_x[None],
                grad_norm_a, grad_wq_a, grad_wkv_a[:, :kv_cols], grad_wkv_a[:, kv_cols:], grad_wo_a,
                grad_norm_b, grad_wq_b, grad_wkv_b[:, :kv_cols], grad_wkv_b[:, kv_cols:], grad_wo_b)

    return jax.shard_map(body, mesh=mesh, in_specs=in_specs, out_specs=out_specs, check_vma=False)
```

time: 2030 us -> 1000 us (0.49)
  waiting for transfers between devices: 1190 us -> 384 us
  matrix products: 486 us -> 124 us
  Pallas kernels: 0 us -> 207 us
  other arithmetic: 194 us -> 63.6 us
  local copies, waits for them, and re-layouts: 60.4 us -> 113 us
  starting transfers between devices: 48.8 us -> 85.4 us
  blocking collectives: 24.7 us -> 0 us
    reduce_scatter x8 -> x2, waiting for transfers between devices: 720 us -> 44.1 us  [scatter_kv(): return lax.psum_scatter(grad, 'cp', scatter_dimension=0, tiled=True)]
    dot_general x36 -> x16, matrix products: 486 us -> 124 us  [dot(): lax.dot_general(lhs, rhs, (((lhs_dim,), (rhs_dim,)), ((), ())), preferred...]
    psum x2 -> x4, waiting for transfers between devices: 290 us -> 73.9 us  [the longest x1 32.3 us: body(): attn_b_lo = lax.psum(attn_b[:half], 'tp')]
    ppermute x28 -> x80, waiting for transfers between devices: 24.6 us -> 239 us  [the longest x76 237 us: swap(): lax.ppermute(val, 'cp', [(source, source ^ mask) for source in range(cp_s...]
    pallas_call x0 -> x10, Pallas kernels: none -> 207 us  [the longest x2 82.3 us: attn_backward(): pl.pallas_call(functools.partial(attn_bwd_kernel, local, scale * LOG2E, s...]
    psum x1, waiting for transfers between devices: 133 us -> 1.14 us  [body(): attn_a = lax.psum(project(out_a, wo_a), 'tp')]
    another operation x2, other arithmetic: 77.5 us -> 0.15 us  [the longest x1 0.08 us: body(): info_b = jnp.stack([cp_rank, jnp.zeros_like(cp_rank)]).astype(jnp.int32)]
    reduce_sum x4 -> x3, other arithmetic: 50.7 us -> 15.4 us  [the longest x2 10.2 us: norm_backward(): jnp.mean(grad_hat * x_hat, axis=-1, keepdims=True)]
  transfers between devices with their start and end apart: 43 -> 91, of which waited for: 16 -> 26; matrix products, arithmetic and copies ran while one was open for 26% -> 16% of each run, Pallas kernels for 0% -> 18%
where the time goes in v1:
time: 1000 us; the launch traced here: 993 us
  waiting for transfers between devices  384 us (38%)
  Pallas kernels  207 us (21%)
  matrix products  124 us (12%)
  local copies, waits for them, and re-layouts  113 us (11%)
  starting transfers between devices  85.4 us (9%)
  other arithmetic  63.6 us (6%)
  between operations  16 us (2%)
    ppermute x76, waiting for transfers between devices, swap(): lax.ppermute(val, 'cp', [(source, source ^ mask) for source in range(cp_s...  237 us
    dot_general x16, matrix products, dot(): lax.dot_general(lhs, rhs, (((lhs_dim,), (rhs_dim,)), ((), ())), preferred...  124 us
    pallas_call x2, Pallas kernels, attn_backward(): pl.pallas_call(functools.partial(attn_bwd_kernel, local, scale * LOG2E, s...  82.3 us
    unnamed x291, local copies, waits for them, and re-layouts  68.6 us
    ppermute x76, starting transfers between devices, swap(): lax.ppermute(val, 'cp', [(source, source ^ mask) for source in range(cp_s...  67.5 us
    pallas_call x2, Pallas kernels, attn_forward(): pl.pallas_call(functools.partial(attn_fwd_kernel, local, scale * LOG2E),...  65.3 us
    pallas_call x6, Pallas kernels, weight_grad(): pl.pallas_call(functools.partial(wgrad_kernel, n_blocks, flip), out_shape...  59.7 us
    reduce_scatter x2, waiting for transfers between devices, scatter_kv(): return lax.psum_scatter(grad, 'cp', scatter_dimension=0, tiled=True)  44.1 us
  transfers between devices with their start and end apart: 91, of which 26 were waited for; matrix products, arithmetic and copies ran while one was open for 16% of the time, Pallas kernels for 18%

profile of v1, /device:TPU:0, one launch (start us, length us, event | category | flops | bytes accessed | tf_op | source)
XLA Modules:
  0.0 993.0 jit_solution(3206079296159591718)
XLA Ops:
  7.3 3.1 fusion.24
  30.1 3.3 copy.72
  33.4 12.1 %fusion.35 = f32[384,1280]{1,0:T(8,128)} fusion(bf16[384,5120]{1,0:T(8,128)(2,1)} %copy-done.101, bf16[5120,1280]{1,0:T(8,128)(2,1)} %param.20), kind=kOutput, calls=%fused_computation.49 | convolution fusion | flops 5034147840 | bytes 19005440 | tf_op jit(solution)/shard_map/dot_general | solution.py:48
  45.5 2.9 copy.73
  53.3 2.9 copy.75
  57.6 2.9 copy.76
  60.6 4.7 multiply_convert_fusion.1.q_ref
  68.4 32.6 %attn_fwd_a.1 = (bf16[384,1280]{1,0:T(8,128)(2,1)S(1)}, f32[10,1,384]{2,1,0:T(1,128)S(1)}) custom-call(s32[2]{0:T(128)S(1)} %pad_add_fusion.info, bf16[384,1280]{1,0:T(8,128)(2,1)S(1)} %copy-done.6, bf16[3072,512]{1,0:T(8,128)(2,1)S(1)} %copy-done.46, bf16[3072,512]{1,0:T(8,128)(2,1)S(1)} %copy-done.46), custom_call_target="tpu_custom_call" | custom-call | flops 24159191040 | bytes 8388608 | tf_op jit(solution)/shard_map/attn_fwd_a/pallas_call | solution.py:155
  102.0 6.8 convolution_convert_fusion.1
  111.7 3.6 collective-permute-start.13
  116.1 2.9 collective-permute-start.9
  118.9 8.0 collective-permute-done.13.refs_7_
  130.6 7.6 collective-permute-done.12.refs_6_
  143.0 5.9 collective-permute-done.9.refs_3_
  149.7 9.6 collective-permute-done.8.refs_2_
  163.7 5.4 collective-permute-done.6.refs_7_
  172.0 8.3 collective-permute-done.4.refs_5_
  184.0 7.1 collective-permute-done.2.refs_3_
  193.5 43.2 %collective-permute-done.1.refs_2_ = bf16[384,640]{1,0:T(8,128)(2,1)S(1)} collective-permute-done((bf16[384,640]{1,0:T(8,128)(2,1)S(1)}, bf16[384,640]{1,0:T(8,128)(2,1)S(1)}, u32[]{:S(2)}, u32[]{:S(2)}) %collective-permute-start.1) | collective-permute-done | bytes 491552 | tf_op jit(solution)/shard_map/ppermute | solution.py:240
  238.6 5.1 collective-permute-done.refs_1_
  245.5 9.4 fusion.29.do_ref
  257.9 5.1 fusion.15
  270.5 11.6 %fusion.34.q_ref = bf16[384,1280]{1,0:T(8,128)(2,1)} fusion(bf16[384,5120]{1,0:T(8,128)(2,1)} %copy-done.102, bf16[5120,1280]{1,0:T(8,128)(2,1)} %param.25, f32[384]{0:T(512)S(1)} %fusion.47), kind=kOutput, calls=%fused_computation.47 | convolution fusion | flops 5035130880 | bytes 18023936 | tf_op jit(solution)/shard_map/dot_general | solution.py:48
  282.1 19.4 %all-gather.5.cloned.1.call-done.k_ref.v_ref = bf16[3072,512]{1,0:T(8,128)(2,1)} async-done(((bf16[384,512]{1,0:T(8,128)(2,1)}), bf16[3072,512]{1,0:T(8,128)(2,1)}) %all-gather.5.cloned.1.call-update) | async-done | bytes 3145744 | tf_op jit(solution)/shard_map/all_gather | solution.py:296
  301.5 3.4 constant_dynamic-slice_fusion.8
  309.7 32.6 %attn_fwd_b.1 = (bf16[384,1280]{1,0:T(8,128)(2,1)S(1)}, f32[10,1,384]{2,1,0:T(1,128)S(1)}) custom-call(s32[2]{0:T(128)S(1)} %pad_add_fusion.1.info, bf16[384,1280]{1,0:T(8,128)(2,1)S(1)} %copy-done.88, bf16[3072,512]{1,0:T(8,128)(2,1)S(1)} %copy-done.48, bf16[3072,512]{1,0:T(8,128)(2,1)S(1)} %copy-done.48), custom_call_target="tpu_custom_call" | custom-call | flops 24159191040 | bytes 8388608 | tf_op jit(solution)/shard_map/attn_fwd_b/pallas_call | solution.py:155
  344.5 10.2 %convolution_convert_fusion = bf16[384,5120]{1,0:T(8,128)(2,1)S(1)} fusion(bf16[384,1280]{1,0:T(8,128)(2,1)S(1)} %get-tuple-element.89.o_ref.refs_8_, bf16[1280,5120]{1,0:T(8,128)(2,1)} %param.28), kind=kOutput, calls=%fused_computation.36 | convolution fusion | flops 5035130880 | bytes 18022400 | tf_op jit(solution)/shard_map/dot_general | solution.py:48
  367.1 40.4 %attn_bwd_b.1 = (f32[384,1280]{1,0:T(8,128)S(1)}, bf16[3072,512]{1,0:T(8,128)(2,1)S(1)}) custom-call(s32[2]{0:T(128)S(1)} %pad_add_fusion.1.info, bf16[384,1280]{1,0:T(8,128)(2,1)S(1)} %copy-done.89, bf16[3072,512]{1,0:T(8,128)(2,1)S(1)} %copy-done.49, bf16[3072,512]{1,0:T(8,128)(2,1)S(1)} %copy-done.49, bf16[384,1280]{1,0:T(8,128)(2,1)S(1)} %copy-done.57, ...), custom_call_target="tpu_custom_call" | custom-call | flops 60397977600 | bytes 12582912 | tf_op jit(solution)/shard_map/attn_bwd_b/pallas_call | solution.py:177
  410.6 32.3 %all-reduce.12.cloned.1.call-done = bf16[192,5120]{1,0:T(8,128)(2,1)} async-done(((bf16[192,5120]{1,0:T(8,128)(2,1)}), bf16[192,5120]{1,0:T(8,128)(2,1)}) %all-reduce.12.cloned.1.call-update) | async-done | bytes 1966096 | tf_op jit(solution)/shard_map/psum | solution.py:324
  448.2 19.9 %fusion.58 = f32[384,5120]{1,0:T(8,128)} fusion(bf16[384,1280]{1,0:T(8,128)(2,1)S(1)} %multiply_convert_fusion.refs_8_, bf16[5120,1280]{1,0:T(8,128)(2,1)} %param.25), kind=kOutput, calls=%fused_computation.157 | convolution fusion | flops 5033164800 | bytes 21954560 | tf_op jit(solution)/shard_map/dot_general | solution.py:48
  468.0 23.2 %reduce-scatter.3.cloned.1.call-done.refs_8_ = bf16[384,512]{1,0:T(8,128)(2,1)} async-done(((bf16[3072,512]{1,0:T(8,128)(2,1)}), bf16[384,512]{1,0:T(8,128)(2,1)}) %reduce-scatter.3.cloned.1.call-update) | async-done | bytes 393232 | tf_op jit(solution)/shard_map/reduce_scatter | solution.py:299
  491.3 3.2 fusion.39
  494.5 6.4 fusion.9
  507.2 39.2 %collective-permute-done.29.refs_10_ = bf16[384,1280]{1,0:T(8,128)(2,1)} collective-permute-done((bf16[384,1280]{1,0:T(8,128)(2,1)S(1)}, bf16[384,1280]{1,0:T(8,128)(2,1)}, u32[]{:S(2)}, u32[]{:S(2)}) %collective-permute-start.29) | collective-permute-done | bytes 983072 | tf_op jit(solution)/shard_map/ppermute | solution.py:240
  548.4 19.4 %collective-permute-done.49 = f32[2560]{0:T(1024)S(1)} collective-permute-done((f32[2560]{0:T(1024)S(1)}, f32[2560]{0:T(1024)S(1)}, u32[]{:S(2)}, u32[]{:S(2)}) %collective-permute-start.49) | collective-permute-done | bytes 10272 | tf_op jit(solution)/shard_map/ppermute | solution.py:240
  572.4 2.8 collective-permute-done.51
  590.2 12.1 %shard_map.238 = bf16[1280,640]{1,0:T(8,128)(2,1)} custom-call(bf16[384,640]{1,0:T(8,128)(2,1)S(1)} %copy-done.12, bf16[384,640]{1,0:T(8,128)(2,1)S(1)} %copy-done.71, bf16[384,640]{1,0:T(8,128)(2,1)S(1)} %copy-done.69, bf16[384,640]{1,0:T(8,128)(2,1)S(1)} %copy-done.67, bf16[384,640]{1,0:T(8,128)(2,1)S(1)} %copy-done.65, bf16[384,640]{1,0:T(8,128)(2,1)S(1)} %copy-done.63, ...), custom_call_target="tpu_custom_call" | custom-call | flops 5033164800 | bytes 16777216 | tf_op jit(solution)/shard_map/pallas_call | solution.py:213
  605.5 11.1 %shard_map.239 = bf16[640,1280]{1,0:T(8,128)(2,1)} custom-call(bf16[384,640]{1,0:T(8,128)(2,1)S(1)} %copy-done.4, bf16[384,640]{1,0:T(8,128)(2,1)S(1)} %copy-done.41, bf16[384,640]{1,0:T(8,128)(2,1)S(1)} %copy-done.39, bf16[384,640]{1,0:T(8,128)(2,1)S(1)} %copy-done.37, bf16[384,640]{1,0:T(8,128)(2,1)S(1)} %copy-done.35, bf16[384,640]{1,0:T(8,128)(2,1)S(1)} %copy-done.33, ...), custom_call_target="tpu_custom_call" | custom-call | flops 5033164800 | bytes 16777216 | tf_op jit(solution)/shard_map/pallas_call | solution.py:213
  617.3 6.3 shard_map.240
  623.6 24.1 %all-reduce.14.cloned.1.call-done = bf16[384,5120]{1,0:T(8,128)(2,1)} async-done(((bf16[384,5120]{1,0:T(8,128)(2,1)}), bf16[384,5120]{1,0:T(8,128)(2,1)}) %all-reduce.14.cloned.1.call-update) | async-done | bytes 3932176 | tf_op jit(solution)/shard_map/psum | solution.py:335
  647.8 5.1 fusion.10
  653.4 4.7 fusion.14
  662.8 9.6 convolution_convert_fusion.2.do_ref
  677.6 7.7 collective-permute-done.59.refs_6_
  689.7 41.9 %attn_bwd_a.1 = (bf16[384,1280]{1,0:T(8,128)(2,1)S(1)}, bf16[3072,512]{1,0:T(8,128)(2,1)}) custom-call(s32[2]{0:T(128)S(1)} %copy-done.85, bf16[384,1280]{1,0:T(8,128)(2,1)S(1)} %copy-done.7, bf16[3072,512]{1,0:T(8,128)(2,1)S(1)} %copy-done.47, bf16[3072,512]{1,0:T(8,128)(2,1)S(1)} %copy-done.47, bf16[384,1280]{1,0:T(8,128)(2,1)S(1)} %copy-done.52, ...), custom_call_target="tpu_custom_call" | custom-call | flops 60397977600 | bytes 12582912 | tf_op jit(solution)/shard_map/attn_bwd_a/pallas_call | solution.py:177
  736.5 17.4 %all-reduce.16.cloned.1.call-done = bf16[192,5120]{1,0:T(8,128)(2,1)} async-done(((bf16[192,5120]{1,0:T(8,128)(2,1)}), bf16[192,5120]{1,0:T(8,128)(2,1)}) %all-reduce.16.cloned.1.call-update) | async-done | bytes 1966096 | tf_op jit(solution)/shard_map/psum | solution.py:341
  754.0 2.9 copy.83
  761.5 20.6 %fusion.59 = f32[384,5120]{1,0:T(8,128)} fusion(bf16[384,1280]{0,1:T(8,128)(2,1)S(1)} %bitcast.106, bf16[5120,1280]{1,0:T(8,128)(2,1)} %param.20), kind=kOutput, calls=%fused_computation.158 | convolution fusion | flops 5033164800 | bytes 21954560 | tf_op jit(solution)/shard_map/dot_general | solution.py:48
  782.1 20.9 %reduce-scatter.5.cloned.1.call-done = bf16[384,512]{1,0:T(8,128)(2,1)} async-done(((bf16[3072,512]{1,0:T(8,128)(2,1)}), bf16[384,512]{1,0:T(8,128)(2,1)}) %reduce-scatter.5.cloned.1.call-update) | async-done | bytes 393232 | tf_op jit(solution)/shard_map/reduce_scatter | solution.py:299
  810.4 7.2 fusion.18
  828.3 12.1 %shard_map.241 = bf16[1280,640]{1,0:T(8,128)(2,1)} custom-call(bf16[384,640]{1,0:T(8,128)(2,1)S(1)} %get-tuple-element.122.refs_0_, bf16[384,640]{1,0:T(8,128)(2,1)S(1)} %copy-done.83, bf16[384,640]{1,0:T(8,128)(2,1)S(1)} %copy-done.81, bf16[384,640]{1,0:T(8,128)(2,1)S(1)} %copy-done.79, bf16[384,640]{1,0:T(8,128)(2,1)S(1)} %copy-done.77, ...), custom_call_target="tpu_custom_call" | custom-call | flops 5033164800 | bytes 16777216 | tf_op jit(solution)/shard_map/pallas_call | solution.py:213
  840.4 4.6 all-to-all-start
  845.8 2.9 collective-permute-start.70
  860.7 15.0 %collective-permute-done.70.refs_11_ = bf16[384,512]{1,0:T(8,128)(2,1)S(1)} collective-permute-done((bf16[384,512]{1,0:T(8,128)(2,1)S(1)}, bf16[384,512]{1,0:T(8,128)(2,1)S(1)}, u32[]{:S(2)}, u32[]{:S(2)}) %collective-permute-start.70) | collective-permute-done | bytes 393248 | tf_op jit(solution)/shard_map/ppermute | solution.py:240
  876.3 48.5 %collective-permute-done.69.refs_10_ = bf16[384,512]{1,0:T(8,128)(2,1)} collective-permute-done((bf16[384,512]{1,0:T(8,128)(2,1)S(1)}, bf16[384,512]{1,0:T(8,128)(2,1)}, u32[]{:S(2)}, u32[]{:S(2)}) %collective-permute-start.69) | collective-permute-done | bytes 393248 | tf_op jit(solution)/shard_map/ppermute | solution.py:240
  928.0 4.3 all-to-all-start.1
  933.5 5.0 fusion.16
  938.5 2.8 copy.97
  941.9 6.5 shard_map.243
  948.4 5.6 all-to-all-done.1
  954.0 2.8 copy.98
  962.0 11.6 %shard_map.242 = bf16[640,1280]{1,0:T(8,128)(2,1)} custom-call(bf16[384,640]{1,0:T(8,128)(2,1)S(1)} %get-tuple-element.138.refs_0_, bf16[384,640]{1,0:T(8,128)(2,1)S(1)} %copy-done.27, bf16[384,640]{1,0:T(8,128)(2,1)S(1)} %copy-done.24, bf16[384,640]{1,0:T(8,128)(2,1)S(1)} %copy-done.21, bf16[384,640]{1,0:T(8,128)(2,1)S(1)} %copy-done.18, ...), custom_call_target="tpu_custom_call" | custom-call | flops 5033164800 | bytes 16777216 | tf_op jit(solution)/shard_map/pallas_call | solution.py:213
  973.7 5.1 fusion.19
  979.3 6.1 fusion.26
  (528 shorter events, 195.9 us)
Async XLA Ops:
  7.2 58.1 %all-gather.3.cloned.1.call-start = ((), (), s32[]{:S(2)}) async-start(), calls=%async_computation.4 | async-start | bytes 3538944 | tf_op jit(solution)/shard_map/all_gather | solution.py:296
  27.1 230.8 %all-reduce.10.cloned.1.call-start = ((), (), s32[]{:S(2)}) async-start(), calls=%async_computation.5 | async-start | bytes 7864320 | tf_op jit(solution)/shard_map/psum | solution.py:308
  108.8 192.7 %all-gather.5.cloned.1.call-start = ((), (), s32[]{:S(2)}) async-start(), calls=%async_computation.6 | async-start | bytes 3538944 | tf_op jit(solution)/shard_map/all_gather | solution.py:296
  115.3 22.9 %collective-permute-start.12 = (bf16[384,640]{1,0:T(8,128)(2,1)S(1)}, bf16[384,640]{1,0:T(8,128)(2,1)}, u32[]{:S(2)}, u32[]{:S(2)}) collective-permute-start(bf16[384,640]{1,0:T(8,128)(2,1)S(1)} %get-tuple-element.185), channel_id=1, source_target_pairs={{0,5},{1,4},{2,7},{3,6},{4,1},{5,0},{6,3},{7,2},{8,13},{9,12},{10,... | collective-permute-start | bytes 1474568 | tf_op jit(solution)/shard_map/ppermute | solution.py:240
  116.0 23.8 %collective-permute-start.11 = (bf16[384,640]{1,0:T(8,128)(2,1)S(1)}, bf16[384,640]{1,0:T(8,128)(2,1)S(1)}, u32[]{:S(2)}, u32[]{:S(2)}) collective-permute-start(bf16[384,640]{1,0:T(8,128)(2,1)S(1)} %get-tuple-element.186), channel_id=1, source_target_pairs={{0,3},{1,2},{2,1},{3,0},{4,7},{5,6},{6,5},{7,4},{8,11},{9,10},{10,... | collective-permute-start | bytes 1474568 | tf_op jit(solution)/shard_map/ppermute | solution.py:240
  116.0 25.8 %collective-permute-start.10 = (bf16[384,640]{1,0:T(8,128)(2,1)S(1)}, bf16[384,640]{1,0:T(8,128)(2,1)S(1)}, u32[]{:S(2)}, u32[]{:S(2)}) collective-permute-start(bf16[384,640]{1,0:T(8,128)(2,1)S(1)} %get-tuple-element.187), channel_id=1, source_target_pairs={{0,1},{1,0},{2,3},{3,2},{4,5},{5,4},{6,7},{7,6},{8,9},{9,8},{10,11... | collective-permute-start | bytes 1474568 | tf_op jit(solution)/shard_map/ppermute | solution.py:240
  116.1 32.8 %collective-permute-start.9 = (bf16[384,640]{1,0:T(8,128)(2,1)S(1)}, bf16[384,640]{1,0:T(8,128)(2,1)S(1)}, u32[]{:S(2)}, u32[]{:S(2)}) collective-permute-start(bf16[384,640]{1,0:T(8,128)(2,1)S(1)} %get-tuple-element.188), channel_id=1, source_target_pairs={{0,6},{1,7},{2,4},{3,5},{4,2},{5,3},{6,0},{7,1},{8,14},{9,15},{10,... | collective-permute-start | bytes 1474568 | tf_op jit(solution)/shard_map/ppermute | solution.py:240
  127.0 32.2 %collective-permute-start.8 = (bf16[384,640]{1,0:T(8,128)(2,1)S(1)}, bf16[384,640]{1,0:T(8,128)(2,1)S(1)}, u32[]{:S(2)}, u32[]{:S(2)}) collective-permute-start(bf16[384,640]{1,0:T(8,128)(2,1)S(1)} %get-tuple-element.189), channel_id=1, source_target_pairs={{0,4},{1,5},{2,6},{3,7},{4,0},{5,1},{6,2},{7,3},{8,12},{9,13},{10,... | collective-permute-start | bytes 1474568 | tf_op jit(solution)/shard_map/ppermute | solution.py:240
  138.2 23.4 %collective-permute-start.7 = (bf16[384,640]{1,0:T(8,128)(2,1)S(1)}, bf16[384,640]{1,0:T(8,128)(2,1)S(1)}, u32[]{:S(2)}, u32[]{:S(2)}) collective-permute-start(bf16[384,640]{1,0:T(8,128)(2,1)S(1)} %get-tuple-element.190), channel_id=1, source_target_pairs={{0,2},{1,3},{2,0},{3,1},{4,6},{5,7},{6,4},{7,5},{8,10},{9,11},{10,... | collective-permute-start | bytes 1474568 | tf_op jit(solution)/shard_map/ppermute | solution.py:240
  140.6 28.5 %collective-permute-start.6 = (bf16[384,640]{1,0:T(8,128)(2,1)S(1)}, bf16[384,640]{1,0:T(8,128)(2,1)S(1)}, u32[]{:S(2)}, u32[]{:S(2)}) collective-permute-start(bf16[384,640]{1,0:T(8,128)(2,1)S(1)} %get-tuple-element.192), channel_id=1, source_target_pairs={{0,7},{1,6},{2,5},{3,4},{4,3},{5,2},{6,1},{7,0},{8,15},{9,14},{10,... | collective-permute-start | bytes 1474568 | tf_op jit(solution)/shard_map/ppermute | solution.py:240
  142.6 37.7 %collective-permute-start.4 = (bf16[384,640]{1,0:T(8,128)(2,1)S(1)}, bf16[384,640]{1,0:T(8,128)(2,1)S(1)}, u32[]{:S(2)}, u32[]{:S(2)}) collective-permute-start(bf16[384,640]{1,0:T(8,128)(2,1)S(1)} %get-tuple-element.193), channel_id=1, source_target_pairs={{0,3},{1,2},{2,1},{3,0},{4,7},{5,6},{6,5},{7,4},{8,11},{9,10},{10,... | collective-permute-start | bytes 1474568 | tf_op jit(solution)/shard_map/ppermute | solution.py:240
  149.6 32.8 %collective-permute-start.3 = (bf16[384,640]{1,0:T(8,128)(2,1)S(1)}, bf16[384,640]{1,0:T(8,128)(2,1)S(1)}, u32[]{:S(2)}, u32[]{:S(2)}) collective-permute-start(bf16[384,640]{1,0:T(8,128)(2,1)S(1)} %get-tuple-element.194), channel_id=1, source_target_pairs={{0,1},{1,0},{2,3},{3,2},{4,5},{5,4},{6,7},{7,6},{8,9},{9,8},{10,11... | collective-permute-start | bytes 1474568 | tf_op jit(solution)/shard_map/ppermute | solution.py:240
  160.0 31.1 %collective-permute-start.2 = (bf16[384,640]{1,0:T(8,128)(2,1)S(1)}, bf16[384,640]{1,0:T(8,128)(2,1)S(1)}, u32[]{:S(2)}, u32[]{:S(2)}) collective-permute-start(bf16[384,640]{1,0:T(8,128)(2,1)S(1)} %get-tuple-element.195), channel_id=1, source_target_pairs={{0,6},{1,7},{2,4},{3,5},{4,2},{5,3},{6,0},{7,1},{8,14},{9,15},{10,... | collective-permute-start | bytes 1474568 | tf_op jit(solution)/shard_map/ppermute | solution.py:240
  162.4 82.1 %collective-permute-start.16 = (bf16[384,1280]{1,0:T(8,128)(2,1)S(1)}, bf16[384,1280]{1,0:T(8,128)(2,1)}, u32[]{:S(2)}, u32[]{:S(2)}) collective-permute-start(bf16[384,1280]{1,0:T(8,128)(2,1)S(1)} %copy-done.51), channel_id=1, source_target_pairs={{0,6},{1,7},{2,4},{3,5},{4,2},{5,3},{6,0},{7,1},{8,14},{9,15},{10,... | collective-permute-start | bytes 2949128 | tf_op jit(solution)/shard_map/ppermute | solution.py:240
  169.9 75.1 %collective-permute-start.15 = (bf16[384,1280]{1,0:T(8,128)(2,1)S(1)}, bf16[384,1280]{1,0:T(8,128)(2,1)}, u32[]{:S(2)}, u32[]{:S(2)}) collective-permute-start(bf16[384,1280]{1,0:T(8,128)(2,1)S(1)} %copy-done.51), channel_id=1, source_target_pairs={{0,4},{1,5},{2,6},{3,7},{4,0},{5,1},{6,2},{7,3},{8,12},{9,13},{10,... | collective-permute-start | bytes 2949128 | tf_op jit(solution)/shard_map/ppermute | solution.py:240
  181.1 64.0 %collective-permute-start.14 = (bf16[384,1280]{1,0:T(8,128)(2,1)S(1)}, bf16[384,1280]{1,0:T(8,128)(2,1)S(1)}, u32[]{:S(2)}, u32[]{:S(2)}) collective-permute-start(bf16[384,1280]{1,0:T(8,128)(2,1)S(1)} %copy-done.51), channel_id=1, source_target_pairs={{0,2},{1,3},{2,0},{3,1},{4,6},{5,7},{6,4},{7,5},{8,10},{9,11},{10,... | collective-permute-start | bytes 2949128 | tf_op jit(solution)/shard_map/ppermute | solution.py:240
  183.2 53.5 %collective-permute-start.1 = (bf16[384,640]{1,0:T(8,128)(2,1)S(1)}, bf16[384,640]{1,0:T(8,128)(2,1)S(1)}, u32[]{:S(2)}, u32[]{:S(2)}) collective-permute-start(bf16[384,640]{1,0:T(8,128)(2,1)S(1)} %get-tuple-element.196), channel_id=1, source_target_pairs={{0,4},{1,5},{2,6},{3,7},{4,0},{5,1},{6,2},{7,3},{8,12},{9,13},{10,... | collective-permute-start | bytes 1474568 | tf_op jit(solution)/shard_map/ppermute | solution.py:240
  191.9 51.9 %collective-permute-start = (bf16[384,640]{1,0:T(8,128)(2,1)S(1)}, bf16[384,640]{1,0:T(8,128)(2,1)S(1)}, u32[]{:S(2)}, u32[]{:S(2)}) collective-permute-start(bf16[384,640]{1,0:T(8,128)(2,1)S(1)} %get-tuple-element.197), channel_id=1, source_target_pairs={{0,2},{1,3},{2,0},{3,1},{4,6},{5,7},{6,4},{7,5},{8,10},{9,11},{10,... | collective-permute-start | bytes 1474568 | tf_op jit(solution)/shard_map/ppermute | solution.py:240
  237.5 17.5 %collective-permute-start.5 = (bf16[384,640]{1,0:T(8,128)(2,1)S(1)}, bf16[384,640]{1,0:T(8,128)(2,1)S(1)}, u32[]{:S(2)}, u32[]{:S(2)}) collective-permute-start(bf16[384,640]{1,0:T(8,128)(2,1)S(1)} %get-tuple-element.199), channel_id=1, source_target_pairs={{0,5},{1,4},{2,7},{3,6},{4,1},{5,0},{6,3},{7,2},{8,13},{9,12},{10,... | collective-permute-start | bytes 1474568 | tf_op jit(solution)/shard_map/ppermute | solution.py:240
  270.2 172.7 %all-reduce.12.cloned.1.call-start = ((), (), s32[]{:S(2)}) async-start(), calls=%async_computation.7 | async-start | bytes 3932160 | tf_op jit(solution)/shard_map/psum | solution.py:324
  304.9 37.4 %collective-permute-start.27 = (bf16[384,640]{1,0:T(8,128)(2,1)S(1)}, bf16[384,640]{1,0:T(8,128)(2,1)S(1)}, u32[]{:S(2)}, u32[]{:S(2)}) collective-permute-start(bf16[384,640]{1,0:T(8,128)(2,1)S(1)} %get-tuple-element.176), channel_id=1, source_target_pairs={{0,7},{1,6},{2,5},{3,4},{4,3},{5,2},{6,1},{7,0},{8,15},{9,14},{10,... | collective-permute-start | bytes 1474568 | tf_op jit(solution)/shard_map/ppermute | solution.py:240
  306.2 37.7 %collective-permute-start.26 = (bf16[384,640]{1,0:T(8,128)(2,1)S(1)}, bf16[384,640]{1,0:T(8,128)(2,1)S(1)}, u32[]{:S(2)}, u32[]{:S(2)}) collective-permute-start(bf16[384,640]{1,0:T(8,128)(2,1)S(1)} %get-tuple-element.177), channel_id=1, source_target_pairs={{0,5},{1,4},{2,7},{3,6},{4,1},{5,0},{6,3},{7,2},{8,13},{9,12},{10,... | collective-permute-start | bytes 1474568 | tf_op jit(solution)/shard_map/ppermute | solution.py:240
  307.6 47.1 %collective-permute-start.25 = (bf16[384,640]{1,0:T(8,128)(2,1)S(1)}, bf16[384,640]{1,0:T(8,128)(2,1)S(1)}, u32[]{:S(2)}, u32[]{:S(2)}) collective-permute-start(bf16[384,640]{1,0:T(8,128)(2,1)S(1)} %get-tuple-element.178), channel_id=1, source_target_pairs={{0,3},{1,2},{2,1},{3,0},{4,7},{5,6},{6,5},{7,4},{8,11},{9,10},{10,... | collective-permute-start | bytes 1474568 | tf_op jit(solution)/shard_map/ppermute | solution.py:240
  308.0 47.6 %collective-permute-start.24 = (bf16[384,640]{1,0:T(8,128)(2,1)S(1)}, bf16[384,640]{1,0:T(8,128)(2,1)S(1)}, u32[]{:S(2)}, u32[]{:S(2)}) collective-permute-start(bf16[384,640]{1,0:T(8,128)(2,1)S(1)} %get-tuple-element.179), channel_id=1, source_target_pairs={{0,1},{1,0},{2,3},{3,2},{4,5},{5,4},{6,7},{7,6},{8,9},{9,8},{10,11... | collective-permute-start | bytes 1474568 | tf_op jit(solution)/shard_map/ppermute | solution.py:240
  308.3 48.7 %collective-permute-start.23 = (bf16[384,640]{1,0:T(8,128)(2,1)S(1)}, bf16[384,640]{1,0:T(8,128)(2,1)S(1)}, u32[]{:S(2)}, u32[]{:S(2)}) collective-permute-start(bf16[384,640]{1,0:T(8,128)(2,1)S(1)} %get-tuple-element.180), channel_id=1, source_target_pairs={{0,6},{1,7},{2,4},{3,5},{4,2},{5,3},{6,0},{7,1},{8,14},{9,15},{10,... | collective-permute-start | bytes 1474568 | tf_op jit(solution)/shard_map/ppermute | solution.py:240
  360.9 130.4 %reduce-scatter.3.cloned.1.call-start = ((), (), s32[]{:S(2)}) async-start(), calls=%async_computation.8 | async-start | bytes 3538944 | tf_op jit(solution)/shard_map/reduce_scatter | solution.py:299
  442.9 204.8 %all-reduce.14.cloned.1.call-start = ((), (), s32[]{:S(2)}) async-start(), calls=%async_computation.9 | async-start | bytes 7864320 | tf_op jit(solution)/shard_map/psum | solution.py:335
  443.0 61.1 %collective-permute-start.31 = (bf16[384,1280]{1,0:T(8,128)(2,1)}, bf16[384,1280]{1,0:T(8,128)(2,1)}, u32[]{:S(2)}, u32[]{:S(2)}) collective-permute-start(bf16[384,1280]{1,0:T(8,128)(2,1)} %copy-done.56), channel_id=1, source_target_pairs={{0,1},{1,0},{2,3},{3,2},{4,5},{5,4},{6,7},{7,6},{8,9},{9,8},{10,11... | collective-permute-start | bytes 2949128 | tf_op jit(solution)/shard_map/ppermute | solution.py:240
  443.1 62.6 %collective-permute-start.30 = (bf16[384,1280]{1,0:T(8,128)(2,1)}, bf16[384,1280]{1,0:T(8,128)(2,1)}, u32[]{:S(2)}, u32[]{:S(2)}) collective-permute-start(bf16[384,1280]{1,0:T(8,128)(2,1)} %copy-done.56), channel_id=1, source_target_pairs={{0,6},{1,7},{2,4},{3,5},{4,2},{5,3},{6,0},{7,1},{8,14},{9,15},{10,... | collective-permute-start | bytes 2949128 | tf_op jit(solution)/shard_map/ppermute | solution.py:240
  500.9 253.0 %all-reduce.16.cloned.1.call-start = ((), (), s32[]{:S(2)}) async-start(), calls=%async_computation.10 | async-start | bytes 3932160 | tf_op jit(solution)/shard_map/psum | solution.py:341
  502.1 44.3 %collective-permute-start.29 = (bf16[384,1280]{1,0:T(8,128)(2,1)S(1)}, bf16[384,1280]{1,0:T(8,128)(2,1)}, u32[]{:S(2)}, u32[]{:S(2)}) collective-permute-start(bf16[384,1280]{1,0:T(8,128)(2,1)S(1)} %copy-done.58), channel_id=1, source_target_pairs={{0,4},{1,5},{2,6},{3,7},{4,0},{5,1},{6,2},{7,3},{8,12},{9,13},{10,... | collective-permute-start | bytes 2949128 | tf_op jit(solution)/shard_map/ppermute | solution.py:240
  503.5 44.3 %collective-permute-start.28 = (bf16[384,1280]{1,0:T(8,128)(2,1)S(1)}, bf16[384,1280]{1,0:T(8,128)(2,1)}, u32[]{:S(2)}, u32[]{:S(2)}) collective-permute-start(bf16[384,1280]{1,0:T(8,128)(2,1)S(1)} %copy-done.58), channel_id=1, source_target_pairs={{0,2},{1,3},{2,0},{3,1},{4,6},{5,7},{6,4},{7,5},{8,10},{9,11},{10,... | collective-permute-start | bytes 2949128 | tf_op jit(solution)/shard_map/ppermute | solution.py:240
  504.1 63.8 %collective-permute-start.38 = (bf16[384,1280]{1,0:T(8,128)(2,1)S(1)}, bf16[384,1280]{1,0:T(8,128)(2,1)}, u32[]{:S(2)}, u32[]{:S(2)}) collective-permute-start(bf16[384,1280]{1,0:T(8,128)(2,1)S(1)} %copy-done.9), channel_id=1, source_target_pairs={{0,1},{1,0},{2,3},{3,2},{4,5},{5,4},{6,7},{7,6},{8,9},{9,8},{10,11... | collective-permute-start | bytes 2949128 | tf_op jit(solution)/shard_map/ppermute | solution.py:240
  504.1 65.3 %collective-permute-start.37 = (bf16[384,1280]{1,0:T(8,128)(2,1)S(1)}, bf16[384,1280]{1,0:T(8,128)(2,1)}, u32[]{:S(2)}, u32[]{:S(2)}) collective-permute-start(bf16[384,1280]{1,0:T(8,128)(2,1)S(1)} %copy-done.9), channel_id=1, source_target_pairs={{0,6},{1,7},{2,4},{3,5},{4,2},{5,3},{6,0},{7,1},{8,14},{9,15},{10,... | collective-permute-start | bytes 2949128 | tf_op jit(solution)/shard_map/ppermute | solution.py:240
  505.7 64.0 %collective-permute-start.36 = (bf16[384,1280]{1,0:T(8,128)(2,1)S(1)}, bf16[384,1280]{1,0:T(8,128)(2,1)}, u32[]{:S(2)}, u32[]{:S(2)}) collective-permute-start(bf16[384,1280]{1,0:T(8,128)(2,1)S(1)} %copy-done.9), channel_id=1, source_target_pairs={{0,4},{1,5},{2,6},{3,7},{4,0},{5,1},{6,2},{7,3},{8,12},{9,13},{10,... | collective-permute-start | bytes 2949128 | tf_op jit(solution)/shard_map/ppermute | solution.py:240
  546.4 21.4 %collective-permute-start.49 = (f32[2560]{0:T(1024)S(1)}, f32[2560]{0:T(1024)S(1)}, u32[]{:S(2)}, u32[]{:S(2)}) collective-permute-start(f32[2560]{0:T(1024)S(1)} %dynamic_slice.181), channel_id=1, source_target_pairs={{0,4},{1,5},{2,6},{3,7},{4,0},{5,1},{6,2},{7,3},{8,12},{9,13},{10,... | collective-permute-start | bytes 30728 | tf_op jit(solution)/shard_map/ppermute | solution.py:240
  547.8 24.0 %collective-permute-start.35 = (bf16[384,1280]{1,0:T(8,128)(2,1)S(1)}, bf16[384,1280]{1,0:T(8,128)(2,1)}, u32[]{:S(2)}, u32[]{:S(2)}) collective-permute-start(bf16[384,1280]{1,0:T(8,128)(2,1)S(1)} %copy-done.9), channel_id=1, source_target_pairs={{0,2},{1,3},{2,0},{3,1},{4,6},{5,7},{6,4},{7,5},{8,10},{9,11},{10,... | collective-permute-start | bytes 2949128 | tf_op jit(solution)/shard_map/ppermute | solution.py:240
  572.3 29.9 %collective-permute-start.40 = (bf16[384,1280]{1,0:T(8,128)(2,1)}, bf16[384,1280]{1,0:T(8,128)(2,1)}, u32[]{:S(2)}, u32[]{:S(2)}) collective-permute-start(bf16[384,1280]{1,0:T(8,128)(2,1)} %collective-permute-done.36.refs_10_), channel_id=1, source_target_pairs={{0,1},{1,0},{2,3},{3,2},{4,5},{5,4},{6,7},{7,6},{8,9},{9,8},{10,11... | collective-permute-start | bytes 2949128 | tf_op jit(solution)/shard_map/ppermute | solution.py:240
  575.2 27.2 %collective-permute-start.39 = (bf16[384,1280]{1,0:T(8,128)(2,1)}, bf16[384,1280]{1,0:T(8,128)(2,1)}, u32[]{:S(2)}, u32[]{:S(2)}) collective-permute-start(bf16[384,1280]{1,0:T(8,128)(2,1)} %collective-permute-done.35.refs_9_), channel_id=1, source_target_pairs={{0,1},{1,0},{2,3},{3,2},{4,5},{5,4},{6,7},{7,6},{8,9},{9,8},{10,11... | collective-permute-start | bytes 2949128 | tf_op jit(solution)/shard_map/ppermute | solution.py:240
  577.0 27.8 %collective-permute-start.44 = (bf16[384,512]{1,0:T(8,128)(2,1)S(1)}, bf16[384,512]{1,0:T(8,128)(2,1)S(1)}, u32[]{:S(2)}, u32[]{:S(2)}) collective-permute-start(bf16[384,512]{1,0:T(8,128)(2,1)S(1)} %copy-done.5), channel_id=1, source_target_pairs={{0,6},{1,7},{2,4},{3,5},{4,2},{5,3},{6,0},{7,1},{8,14},{9,15},{10,... | collective-permute-start | bytes 1179656 | tf_op jit(solution)/shard_map/ppermute | solution.py:240
  578.5 26.5 %collective-permute-start.43 = (bf16[384,512]{1,0:T(8,128)(2,1)S(1)}, bf16[384,512]{1,0:T(8,128)(2,1)S(1)}, u32[]{:S(2)}, u32[]{:S(2)}) collective-permute-start(bf16[384,512]{1,0:T(8,128)(2,1)S(1)} %copy-done.5), channel_id=1, source_target_pairs={{0,4},{1,5},{2,6},{3,7},{4,0},{5,1},{6,2},{7,3},{8,12},{9,13},{10,... | collective-permute-start | bytes 1179656 | tf_op jit(solution)/shard_map/ppermute | solution.py:240
  579.6 25.7 %collective-permute-start.42 = (bf16[384,512]{1,0:T(8,128)(2,1)S(1)}, bf16[384,512]{1,0:T(8,128)(2,1)S(1)}, u32[]{:S(2)}, u32[]{:S(2)}) collective-permute-start(bf16[384,512]{1,0:T(8,128)(2,1)S(1)} %copy-done.5), channel_id=1, source_target_pairs={{0,2},{1,3},{2,0},{3,1},{4,6},{5,7},{6,4},{7,5},{8,10},{9,11},{10,... | collective-permute-start | bytes 1179656 | tf_op jit(solution)/shard_map/ppermute | solution.py:240
  660.1 16.9 %collective-permute-start.60 = (bf16[384,640]{1,0:T(8,128)(2,1)}, bf16[384,640]{1,0:T(8,128)(2,1)}, u32[]{:S(2)}, u32[]{:S(2)}) collective-permute-start(bf16[384,640]{1,0:T(8,128)(2,1)} %get-tuple-element.168), channel_id=1, source_target_pairs={{0,7},{1,6},{2,5},{3,4},{4,3},{5,2},{6,1},{7,0},{8,15},{9,14},{10,... | collective-permute-start | bytes 1474568 | tf_op jit(solution)/shard_map/ppermute | solution.py:240
  661.8 23.6 %collective-permute-start.59 = (bf16[384,640]{1,0:T(8,128)(2,1)}, bf16[384,640]{1,0:T(8,128)(2,1)}, u32[]{:S(2)}, u32[]{:S(2)}) collective-permute-start(bf16[384,640]{1,0:T(8,128)(2,1)} %get-tuple-element.169), channel_id=1, source_target_pairs={{0,5},{1,4},{2,7},{3,6},{4,1},{5,0},{6,3},{7,2},{8,13},{9,12},{10,... | collective-permute-start | bytes 1474568 | tf_op jit(solution)/shard_map/ppermute | solution.py:240
  673.9 129.1 %reduce-scatter.5.cloned.1.call-start = ((), (), s32[]{:S(2)}) async-start(), calls=%async_computation.11 | async-start | bytes 3538944 | tf_op jit(solution)/shard_map/reduce_scatter | solution.py:299
  674.0 58.6 %collective-permute-start.58 = (bf16[384,640]{1,0:T(8,128)(2,1)}, bf16[384,640]{1,0:T(8,128)(2,1)S(1)}, u32[]{:S(2)}, u32[]{:S(2)}) collective-permute-start(bf16[384,640]{1,0:T(8,128)(2,1)} %get-tuple-element.170), channel_id=1, source_target_pairs={{0,3},{1,2},{2,1},{3,0},{4,7},{5,6},{6,5},{7,4},{8,11},{9,10},{10,... | collective-permute-start | bytes 1474568 | tf_op jit(solution)/shard_map/ppermute | solution.py:240
  674.2 59.1 %collective-permute-start.57 = (bf16[384,640]{1,0:T(8,128)(2,1)}, bf16[384,640]{1,0:T(8,128)(2,1)S(1)}, u32[]{:S(2)}, u32[]{:S(2)}) collective-permute-start(bf16[384,640]{1,0:T(8,128)(2,1)} %get-tuple-element.171), channel_id=1, source_target_pairs={{0,1},{1,0},{2,3},{3,2},{4,5},{5,4},{6,7},{7,6},{8,9},{9,8},{10,11... | collective-permute-start | bytes 1474568 | tf_op jit(solution)/shard_map/ppermute | solution.py:240
  674.7 59.4 %collective-permute-start.56 = (bf16[384,640]{1,0:T(8,128)(2,1)}, bf16[384,640]{1,0:T(8,128)(2,1)S(1)}, u32[]{:S(2)}, u32[]{:S(2)}) collective-permute-start(bf16[384,640]{1,0:T(8,128)(2,1)} %get-tuple-element.172), channel_id=1, source_target_pairs={{0,6},{1,7},{2,4},{3,5},{4,2},{5,3},{6,0},{7,1},{8,14},{9,15},{10,... | collective-permute-start | bytes 1474568 | tf_op jit(solution)/shard_map/ppermute | solution.py:240
  677.1 57.9 %collective-permute-start.55 = (bf16[384,640]{1,0:T(8,128)(2,1)}, bf16[384,640]{1,0:T(8,128)(2,1)S(1)}, u32[]{:S(2)}, u32[]{:S(2)}) collective-permute-start(bf16[384,640]{1,0:T(8,128)(2,1)} %get-tuple-element.173), channel_id=1, source_target_pairs={{0,4},{1,5},{2,6},{3,7},{4,0},{5,1},{6,2},{7,3},{8,12},{9,13},{10,... | collective-permute-start | bytes 1474568 | tf_op jit(solution)/shard_map/ppermute | solution.py:240
  685.3 50.4 %collective-permute-start.54 = (bf16[384,640]{1,0:T(8,128)(2,1)}, bf16[384,640]{1,0:T(8,128)(2,1)S(1)}, u32[]{:S(2)}, u32[]{:S(2)}) collective-permute-start(bf16[384,640]{1,0:T(8,128)(2,1)} %get-tuple-element.174), channel_id=1, source_target_pairs={{0,2},{1,3},{2,0},{3,1},{4,6},{5,7},{6,4},{7,5},{8,10},{9,11},{10,... | collective-permute-start | bytes 1474568 | tf_op jit(solution)/shard_map/ppermute | solution.py:240
  754.0 219.7 %all-reduce.18.cloned.1.call-start = ((), (), s32[]{:S(2)}) async-start(), calls=%async_computation.12 | async-start | bytes 7864320 | tf_op jit(solution)/shard_map/psum | solution.py:361
  821.5 23.5 %collective-permute-start.76 = (f32[1280]{0:T(1024)S(1)}, f32[1280]{0:T(1024)S(1)}, u32[]{:S(2)}, u32[]{:S(2)}) collective-permute-start(f32[1280]{0:T(1024)S(1)} %dynamic_slice.197), channel_id=1, source_target_pairs={{0,2},{1,3},{2,0},{3,1},{4,6},{5,7},{6,4},{7,5},{8,10},{9,11},{10,... | collective-permute-start | bytes 15368 | tf_op jit(solution)/shard_map/ppermute | solution.py:240
  840.4 86.8 %all-to-all-start = ((bf16[8,160,640]{2,1,0:T(8,128)(2,1)}), bf16[8,160,640]{2,1,0:T(8,128)(2,1)}, u32[]{:S(2)}, u32[]{:S(2)}) async-start(bf16[8,160,640]{2,1,0:T(8,128)(2,1)} %bitcast.112), calls=%async_computation.2 | async-start | bytes 3276800 | tf_op jit(solution)/shard_map/all_to_all | solution.py:273
  845.8 29.9 %collective-permute-start.70 = (bf16[384,512]{1,0:T(8,128)(2,1)S(1)}, bf16[384,512]{1,0:T(8,128)(2,1)S(1)}, u32[]{:S(2)}, u32[]{:S(2)}) collective-permute-start(bf16[384,512]{1,0:T(8,128)(2,1)S(1)} %pad_maximum_fusion.2.refs_8_), channel_id=1, source_target_pairs={{0,6},{1,7},{2,4},{3,5},{4,2},{5,3},{6,0},{7,1},{8,14},{9,15},{10,... | collective-permute-start | bytes 1179656 | tf_op jit(solution)/shard_map/ppermute | solution.py:240
  856.3 76.5 %collective-permute-start.63 = (bf16[384,1280]{1,0:T(8,128)(2,1)}, bf16[384,1280]{1,0:T(8,128)(2,1)}, u32[]{:S(2)}, u32[]{:S(2)}) collective-permute-start(bf16[384,1280]{1,0:T(8,128)(2,1)} %copy.91.refs_8_), channel_id=1, source_target_pairs={{0,6},{1,7},{2,4},{3,5},{4,2},{5,3},{6,0},{7,1},{8,14},{9,15},{10,... | collective-permute-start | bytes 2949128 | tf_op jit(solution)/shard_map/ppermute | solution.py:240
  856.9 76.0 %collective-permute-start.62 = (bf16[384,1280]{1,0:T(8,128)(2,1)}, bf16[384,1280]{1,0:T(8,128)(2,1)}, u32[]{:S(2)}, u32[]{:S(2)}) collective-permute-start(bf16[384,1280]{1,0:T(8,128)(2,1)} %copy.91.refs_8_), channel_id=1, source_target_pairs={{0,4},{1,5},{2,6},{3,7},{4,0},{5,1},{6,2},{7,3},{8,12},{9,13},{10,... | collective-permute-start | bytes 2949128 | tf_op jit(solution)/shard_map/ppermute | solution.py:240
  858.4 75.0 %collective-permute-start.61 = (bf16[384,1280]{1,0:T(8,128)(2,1)}, bf16[384,1280]{1,0:T(8,128)(2,1)}, u32[]{:S(2)}, u32[]{:S(2)}) collective-permute-start(bf16[384,1280]{1,0:T(8,128)(2,1)} %copy.91.refs_8_), channel_id=1, source_target_pairs={{0,2},{1,3},{2,0},{3,1},{4,6},{5,7},{6,4},{7,5},{8,10},{9,11},{10,... | collective-permute-start | bytes 2949128 | tf_op jit(solution)/shard_map/ppermute | solution.py:240
  859.8 64.9 %collective-permute-start.69 = (bf16[384,512]{1,0:T(8,128)(2,1)S(1)}, bf16[384,512]{1,0:T(8,128)(2,1)}, u32[]{:S(2)}, u32[]{:S(2)}) collective-permute-start(bf16[384,512]{1,0:T(8,128)(2,1)S(1)} %pad_maximum_fusion.2.refs_8_), channel_id=1, source_target_pairs={{0,4},{1,5},{2,6},{3,7},{4,0},{5,1},{6,2},{7,3},{8,12},{9,13},{10,... | collective-permute-start | bytes 1179656 | tf_op jit(solution)/shard_map/ppermute | solution.py:240
  875.7 49.1 %collective-permute-start.68 = (bf16[384,512]{1,0:T(8,128)(2,1)S(1)}, bf16[384,512]{1,0:T(8,128)(2,1)S(1)}, u32[]{:S(2)}, u32[]{:S(2)}) collective-permute-start(bf16[384,512]{1,0:T(8,128)(2,1)S(1)} %pad_maximum_fusion.2.refs_8_), channel_id=1, source_target_pairs={{0,2},{1,3},{2,0},{3,1},{4,6},{5,7},{6,4},{7,5},{8,10},{9,11},{10,... | collective-permute-start | bytes 1179656 | tf_op jit(solution)/shard_map/ppermute | solution.py:240
  927.2 29.7 %collective-permute-start.64 = (bf16[384,1280]{1,0:T(8,128)(2,1)}, bf16[384,1280]{1,0:T(8,128)(2,1)}, u32[]{:S(2)}, u32[]{:S(2)}) collective-permute-start(bf16[384,1280]{1,0:T(8,128)(2,1)} %copy.91.refs_8_), channel_id=1, source_target_pairs={{0,1},{1,0},{2,3},{3,2},{4,5},{5,4},{6,7},{7,6},{8,9},{9,8},{10,11... | collective-permute-start | bytes 2949128 | tf_op jit(solution)/shard_map/ppermute | solution.py:240
  928.0 26.0 %all-to-all-start.1 = ((bf16[8,160,640]{2,1,0:T(8,128)(2,1)}), bf16[8,160,640]{2,1,0:T(8,128)(2,1)}, u32[]{:S(2)}, u32[]{:S(2)}) async-start(bf16[8,160,640]{2,1,0:T(8,128)(2,1)} %bitcast.111), calls=%async_computation.3 | async-start | bytes 3276800 | tf_op jit(solution)/shard_map/all_to_all | solution.py:273
  932.8 24.1 %collective-permute-start.67 = (bf16[384,1280]{1,0:T(8,128)(2,1)}, bf16[384,1280]{1,0:T(8,128)(2,1)}, u32[]{:S(2)}, u32[]{:S(2)}) collective-permute-start(bf16[384,1280]{1,0:T(8,128)(2,1)} %collective-permute-done.63.refs_11_), channel_id=1, source_target_pairs={{0,1},{1,0},{2,3},{3,2},{4,5},{5,4},{6,7},{7,6},{8,9},{9,8},{10,11... | collective-permute-start | bytes 2949128 | tf_op jit(solution)/shard_map/ppermute | solution.py:240
  933.0 23.9 %collective-permute-start.66 = (bf16[384,1280]{1,0:T(8,128)(2,1)}, bf16[384,1280]{1,0:T(8,128)(2,1)}, u32[]{:S(2)}, u32[]{:S(2)}) collective-permute-start(bf16[384,1280]{1,0:T(8,128)(2,1)} %collective-permute-done.62.refs_10_), channel_id=1, source_target_pairs={{0,1},{1,0},{2,3},{3,2},{4,5},{5,4},{6,7},{7,6},{8,9},{9,8},{10,11... | collective-permute-start | bytes 2949128 | tf_op jit(solution)/shard_map/ppermute | solution.py:240
  933.3 23.5 %collective-permute-start.65 = (bf16[384,1280]{1,0:T(8,128)(2,1)}, bf16[384,1280]{1,0:T(8,128)(2,1)}, u32[]{:S(2)}, u32[]{:S(2)}) collective-permute-start(bf16[384,1280]{1,0:T(8,128)(2,1)} %collective-permute-done.61.refs_9_), channel_id=1, source_target_pairs={{0,1},{1,0},{2,3},{3,2},{4,5},{5,4},{6,7},{7,6},{8,9},{9,8},{10,11... | collective-permute-start | bytes 2949128 | tf_op jit(solution)/shard_map/ppermute | solution.py:240
  (171 other events, 1572.4 us)
Sparse Core Ops, SparseCore 0:
  27.2 34.8 all-gather.2
  108.9 148.9 all-reduce.9
  270.3 31.1 all-gather.4
  361.0 81.8 all-reduce.11
  446.1 45.1 reduce-scatter.2
  501.0 146.6 all-reduce.13
  674.0 79.8 all-reduce.15
  757.9 45.1 reduce-scatter.4
  819.3 146.6 all-reduce.17
